TPU v7x, 128 devices: a whole 4x4x4 slice. The times are simulated.
128 devices in a mesh: rep: 2 (over core), dp: 64 (over x, y, z).
Axes of the slice: x: 4, y: 4, z: 4, core: 2. Of those that a mesh axis runs over, the one named last changes fastest.
Arguments:
- x: bfloat16 [128, 2048, 1024], P(('rep', 'dp')), parts along dimension 0
- dy: bfloat16 [128, 2048, 1024], P(('rep', 'dp')), parts along dimension 0
- w_gate: bfloat16 [2, 1024, 2560], P(None, 'dp')
- w_up: bfloat16 [2, 1024, 2560], P(None, 'dp')
- w_down: bfloat16 [2, 2560, 1024], P(None, 'dp')
Outputs:
- output 1: bfloat16 [128, 2048, 1024], P(('rep', 'dp')), parts along dimension 0
- output 2: bfloat16 [4, 1024, 2560], P('rep', 'dp'), parts along dimension 0
- output 3: bfloat16 [4, 1024, 2560], P('rep', 'dp'), parts along dimension 0
- output 4: bfloat16 [4, 2560, 1024], P('rep', 'dp'), parts along dimension 0
There are 2 independent parts. A program takes and returns all parts, laid end to end along the dimension named above; an argument that names none is the same for every part.
All inputs are finite; a program needn't handle non-finite values.
Results may differ from a plain program's by a relative error of at most 0.018.
Values are sent between devices in bfloat16 or wider.
A program may use at most 1.5 GiB of HBM per device.

v0:
```python
import jax
import jax.numpy as jnp
from jax import lax

NAMES = ("w_gate", "w_up", "w_down")


def matmul(a, w):
    return jnp.dot(a, w, preferred_element_type=jnp.float32).astype(jnp.bfloat16)


def normed(h):
    wide = h.astype(jnp.float32)
    scale = lax.rsqrt(jnp.mean(wide**2, -1, keepdims=True) + 1e-6)
    return (wide * scale).astype(jnp.bfloat16)


def layer(h, w):
    a = normed(h)
    gate = jnp.dot(a, w["w_gate"], preferred_element_type=jnp.float32)
    up = jnp.dot(a, w["w_up"], preferred_element_type=jnp.float32)
    return h + matmul((jax.nn.silu(gate) * up).astype(jnp.bfloat16), w["w_down"])


def stack(weights, h):
    for number in range(weights["w_gate"].shape[0]):
        h = layer(h, {name: w[number] for name, w in weights.items()})
    return h


def solution(mesh):
    groups = mesh.shape["rep"]

    def step(x, dy, *weights):
        shape = x.shape
        x, dy = (t.reshape(groups, -1, *t.shape[1:]) for t in (x, dy))

        def of_a_group(x, dy):
            _, back = jax.vjp(stack, dict(zip(NAMES, weights, strict=True)), x)
            by_weights, by_x = back(dy)
            return (by_x, *(by_weights[name] for name in NAMES))

        by_x, *by_weights = jax.vmap(of_a_group)(x, dy)
        return (by_x.reshape(shape), *(t.reshape(-1, *t.shape[2:]) for t in by_weights))

    return step
```

profile of v0, /device:TPU:0, one launch (start us, length us, event | category | flops | bytes accessed | tf_op | source)
XLA Modules:
  0.0 2683.6 jit_solution(8722741961242359971)
XLA Ops:
  24.1 59.2 %all-gather.29.cloned.1.call-done = bf16[1,1024,2560]{2,1,0:T(8,128)(2,1)} async-done(((bf16[1,16,2560]{2,1,0:T(8,128)(2,1)}), bf16[1,1024,2560]{2,1,0:T(8,128)(2,1)}) %all-gather.29.cloned.1.call-update) | async-done | bytes 5242896 | tf_op jit(solution)/vmap(jvp())/squeeze | solution.py:27
  83.3 18.2 fusion.68
  101.5 53.1 %all-gather.31.cloned.1.call-done = bf16[1,1024,2560]{2,1,0:T(8,128)(2,1)} async-done(((bf16[1,16,2560]{2,1,0:T(8,128)(2,1)}), bf16[1,1024,2560]{2,1,0:T(8,128)(2,1)}) %all-gather.31.cloned.1.call-update) | async-done | bytes 5242896 | tf_op jit(solution)/vmap(jvp())/squeeze | solution.py:27
  154.6 18.5 fusion.64
  173.1 15.4 fusion.24
  188.5 37.0 %all-gather.33.cloned.1.call-done = bf16[1,2560,1024]{2,1,0:T(8,128)(2,1)} async-done(((bf16[1,40,1024]{2,1,0:T(8,128)(2,1)}), bf16[1,2560,1024]{2,1,0:T(8,128)(2,1)}) %all-gather.33.cloned.1.call-update) | async-done | bytes 5242896 | tf_op jit(solution)/vmap(jvp())/squeeze | solution.py:27
  225.5 18.1 fusion.40
  244.2 52.5 %all-gather.35.cloned.1.call-done = bf16[1,1024,2560]{2,1,0:T(8,128)(2,1)} async-done(((bf16[1,16,2560]{2,1,0:T(8,128)(2,1)}), bf16[1,1024,2560]{2,1,0:T(8,128)(2,1)}) %all-gather.35.cloned.1.call-update) | async-done | bytes 5242896 | tf_op jit(solution)/vmap(jvp())/squeeze | solution.py:27
  296.7 18.3 fusion.58
  315.0 52.9 %all-gather.39.cloned.1.call-done = bf16[1,1024,2560]{2,1,0:T(8,128)(2,1)} async-done(((bf16[1,16,2560]{2,1,0:T(8,128)(2,1)}), bf16[1,1024,2560]{2,1,0:T(8,128)(2,1)}) %all-gather.39.cloned.1.call-update) | async-done | bytes 5242896 | tf_op jit(solution)/vmap(jvp())/squeeze | solution.py:27
  367.9 18.7 fusion.52
  386.7 22.4 fusion.49
  415.9 22.7 all-gather.37.cloned.1.call-done
  438.6 14.4 convolution_convert_fusion.1
  456.9 20.2 fusion.4
  477.1 20.0 fusion.22
  497.1 17.5 fusion.42
  520.4 16.7 convolution_bitcast_fusion
  537.1 20.9 fusion.43
  558.1 14.7 convolution_convert_fusion
  576.6 20.2 fusion.7
  596.8 20.0 fusion.18
  616.9 18.7 fusion.38
  635.6 21.1 fusion.46
  657.4 17.4 convolution_bitcast_fusion.2
  674.9 17.6 convolution_bitcast_fusion.1
  706.5 107.8 %reduce-scatter.27.cloned.1.call-done = f32[1,40,1024]{2,1,0:T(8,128)} async-done(((f32[1,2560,1024]{2,1,0:T(8,128)}), f32[1,40,1024]{2,1,0:T(8,128)}) %reduce-scatter.27.cloned.1.call-update) | async-done | bytes 163856
  815.2 371.3 %reduce-scatter.29.cloned.1.call-done = f32[1,40,1024]{2,1,0:T(8,128)} async-done(((f32[1,2560,1024]{2,1,0:T(8,128)}), f32[1,40,1024]{2,1,0:T(8,128)}) %reduce-scatter.29.cloned.1.call-update) | async-done | bytes 163856
  1188.1 370.3 %reduce-scatter.23.cloned.1.call-done = f32[1,16,2560]{2,1,0:T(8,128)} async-done(((f32[1,1024,2560]{2,1,0:T(8,128)}), f32[1,16,2560]{2,1,0:T(8,128)}) %reduce-scatter.23.cloned.1.call-update) | async-done | bytes 163856
  1559.3 370.9 %reduce-scatter.25.cloned.1.call-done = f32[1,16,2560]{2,1,0:T(8,128)} async-done(((f32[1,1024,2560]{2,1,0:T(8,128)}), f32[1,16,2560]{2,1,0:T(8,128)}) %reduce-scatter.25.cloned.1.call-update) | async-done | bytes 163856
  1931.8 370.7 %reduce-scatter.19.cloned.1.call-done = f32[1,16,2560]{2,1,0:T(8,128)} async-done(((f32[1,1024,2560]{2,1,0:T(8,128)}), f32[1,16,2560]{2,1,0:T(8,128)}) %reduce-scatter.19.cloned.1.call-update) | async-done | bytes 163856
  2303.4 371.3 %reduce-scatter.21.cloned.1.call-done = f32[1,16,2560]{2,1,0:T(8,128)} async-done(((f32[1,1024,2560]{2,1,0:T(8,128)}), f32[1,16,2560]{2,1,0:T(8,128)}) %reduce-scatter.21.cloned.1.call-update) | async-done | bytes 163856
  (71 shorter events, 60.2 us)
Async XLA Ops:
  7.2 76.1 %all-gather.29.cloned.1.call-start = ((), (), s32[]{:S(2)}) async-start(), calls=%async_computation.6 | async-start | bytes 5324800 | tf_op jit(solution)/vmap(jvp())/squeeze | solution.py:27
  8.8 145.8 %all-gather.31.cloned.1.call-start = ((), (), s32[]{:S(2)}) async-start(), calls=%async_computation.7 | async-start | bytes 5324800 | tf_op jit(solution)/vmap(jvp())/squeeze | solution.py:27
  10.5 214.9 %all-gather.33.cloned.1.call-start = ((), (), s32[]{:S(2)}) async-start(), calls=%async_computation.8 | async-start | bytes 5324800 | tf_op jit(solution)/vmap(jvp())/squeeze | solution.py:27
  12.2 284.5 %all-gather.35.cloned.1.call-start = ((), (), s32[]{:S(2)}) async-start(), calls=%async_computation.9 | async-start | bytes 5324800 | tf_op jit(solution)/vmap(jvp())/squeeze | solution.py:27
  12.8 355.2 %all-gather.39.cloned.1.call-start = ((), (), s32[]{:S(2)}) async-start(), calls=%async_computation.11 | async-start | bytes 5324800 | tf_op jit(solution)/vmap(jvp())/squeeze | solution.py:27
  13.4 425.2 %all-gather.37.cloned.1.call-start = ((), (), s32[]{:S(2)}) async-start(), calls=%async_computation.10 | async-start | bytes 5324800 | tf_op jit(solution)/vmap(jvp())/squeeze | solution.py:27
  13.9 800.3 %reduce-scatter.27.cloned.1.call-start = ((), (), s32[]{:S(2)}) async-start(), calls=%async_computation.16 | async-start | bytes 10649600
  154.6 18.5 copy-start
  243.6 0.6 copy-start.6
  244.2 123.8 %copy-start.8 = (f32[1,1,2048]{2,1,0:T(1,128)}, f32[1,1,2048]{2,1,0:T(1,128)S(1)}, u32[]{:S(2)}) copy-start(f32[1,1,2048]{2,1,0:T(1,128)S(1)} %rsqrt.23) | copy-start | bytes 24580
  409.1 777.4 %reduce-scatter.29.cloned.1.call-start = ((), (), s32[]{:S(2)}) async-start(), calls=%async_computation.17 | async-start | bytes 10649600
  453.0 3.9 copy-start.3
  497.1 17.5 copy-start.7
  497.1 17.6 copy-start.2
  497.1 17.6 copy-start.5
  497.1 17.6 copy-start.9
  518.3 2.0 copy-start.1
  537.0 1021.3 %reduce-scatter.23.cloned.1.call-start = ((), (), s32[]{:S(2)}) async-start(), calls=%async_computation.14 | async-start | bytes 10649600
  558.0 1372.2 %reduce-scatter.25.cloned.1.call-start = ((), (), s32[]{:S(2)}) async-start(), calls=%async_computation.15 | async-start | bytes 10649600
  572.8 3.8 copy-start.4
  616.9 18.7 copy-start.11
  656.7 0.7 copy-start.10
  656.8 1645.7 %reduce-scatter.19.cloned.1.call-start = ((), (), s32[]{:S(2)}) async-start(), calls=%async_computation.12 | async-start | bytes 10649600
  674.8 1999.9 %reduce-scatter.21.cloned.1.call-start = ((), (), s32[]{:S(2)}) async-start(), calls=%async_computation.13 | async-start | bytes 10649600
Sparse Core Ops, SparseCore 0:
  10.8 72.3 all-gather.28
  86.7 67.8 all-gather.30
  157.5 67.8 all-gather.32
  228.8 67.8 all-gather.34
  300.0 67.8 all-gather.38
  370.7 67.8 all-gather.36
  441.0 373.2 reduce-scatter.26
  816.7 369.8 reduce-scatter.28
  1188.9 369.4 reduce-scatter.22
  1560.6 369.5 reduce-scatter.24
  1932.6 369.8 reduce-scatter.18
  2304.7 369.9 reduce-scatter.20
where the time goes:
time: 2690 us; the launch traced here: 2680 us
  waiting for transfers between devices  2240 us (83%)
  matrix products  313 us (12%)
  other arithmetic  78.4 us (3%)
  local copies, waits for them, and re-layouts  35.4 us (1%)
    unnamed x18, waiting for transfers between devices  1960 us
    squeeze x6, waiting for transfers between devices, stack(): h = layer(h, {name: w[number] for name, w in weights.items()})  277 us
    dot_general x6, matrix products, layer(): up = jnp.dot(a, w['w_up'], preferred_element_type=jnp.float32)  119 us
    dot_general x6, matrix products, layer(): gate = jnp.dot(a, w['w_gate'], preferred_element_type=jnp.float32)  108 us
    dot_general x5, matrix products, matmul(): jnp.dot(a, w, preferred_element_type=jnp.float32).astype(jnp.bfloat16)  86.3 us
    unnamed x3, other arithmetic  55.8 us
  transfers between devices with their start and end apart: 12, of which 12 were waited for; matrix products, arithmetic and copies ran while one was open for 15% of the time, Pallas kernels for 0%

commit v1 on v0

v1 whole, which is shorter than its diff:
```python
import functools

import jax
import jax.numpy as jnp
from jax import lax
from jax.experimental import pallas as pl
from jax.experimental.pallas import tpu as pltpu
from jax.sharding import PartitionSpec as P

NAMES = ("w_gate", "w_up", "w_down")
MESH = pl.DeviceIdType.MESH
BF, F32 = jnp.bfloat16, jnp.float32
ANY = pl.BlockSpec(memory_space=pl.ANY)
VM = pl.BlockSpec(memory_space=pltpu.VMEM)

GATHER_ORDERS = ((2, 1, 0), (0, 2, 1), (1, 0, 2))
SCATTER_ORDERS = ((0, 1, 2), (1, 2, 0), (2, 0, 1))


def thirds(n):
    tiles = n // 128
    cuts = [0, (tiles + 2) // 3, (tiles + 2) // 3 + (tiles + 1) // 3, tiles]
    return [(cuts[i] * 128, cuts[i + 1] * 128) for i in range(3)]


class Place:
    def __init__(self):
        self.core = lax.axis_index("rep")
        me = lax.axis_index("dp")
        self.at = (me // 16, (me // 4) % 4, me % 4)

    def along(self, axis, step):
        return (self.at[axis] + (step + 4)) % 4

    def peer(self, axis, step):
        x, y, z = (self.along(a, step) if a == axis else self.at[a] for a in range(3))
        return {"dp": (x * 4 + y) * 4 + z}

    def other(self):
        return {"rep": 1 - self.core}


def enter(place, steps, other):
    barrier = pltpu.get_barrier_semaphore()
    for axis in range(3):
        for step in steps:
            pl.semaphore_signal(barrier, inc=1, device_id=place.peer(axis, step), device_id_type=MESH)
    if other:
        pl.semaphore_signal(barrier, inc=1, device_id=place.other(), device_id_type=MESH)
    pl.semaphore_wait(barrier, 3 * len(steps) + other)


class Gather:
    def __init__(self, place, full, mine, parts, send, recv):
        self.p, self.full, self.mine, self.parts, self.send, self.recv = place, full, mine, parts, send, recv
        self.copies = {}

    def view(self, color, where):
        at = [where.get(a, self.p.at[a]) for a in range(3)]
        return self.full.at[(*at, *self.parts[color])]

    def go(self, color, slot, src, dst, device):
        copy = pltpu.make_async_remote_copy(
            src_ref=src, dst_ref=dst, send_sem=self.send.at[color, slot], recv_sem=self.recv.at[color, slot], device_id=device, device_id_type=MESH
        )
        copy.start()
        self.copies[color, slot] = copy

    def stage(self, number):
        for color, (a, b, c) in enumerate(GATHER_ORDERS):
            got = lambda *slots: [self.copies[color, s].wait_recv() for s in slots]
            everything = slice(None)
            if number == 0:
                for slot, step in enumerate((1, -1, 2)):
                    self.go(color, slot, self.mine.at[self.parts[color]], self.view(color, {}), self.p.peer(a, step))
            for first, axis, begin, done in ((3, b, 1, {a: everything}), (7, c, 3, {a: everything, b: everything})):
                if number == begin:
                    if first == 3:
                        got(0, 1, 2)
                    else:
                        got(5, 6)
                    block = self.view(color, done)
                    for slot, step in ((first, 1), (first + 1, -1)):
                        self.go(color, slot, block, block, self.p.peer(axis, step))
                    if first == 7:
                        self.go(color, 11, block, block, self.p.other())
                if number == begin + 1:
                    for slot, step, half in ((first, 1, slice(0, 2)), (first + 1, -1, slice(2, 4))):
                        got(slot)
                        whole = self.view(color, {**done, axis: self.p.along(axis, -step)})
                        part = self.view(color, {**done, axis: self.p.along(axis, -step), a if first == 3 else b: half})
                        self.go(color, slot + 2, part, part, self.p.peer(axis, step))
                        if first == 7:
                            self.go(color, slot + 5, whole, whole, self.p.other())
            if number == 5:
                for slot, step, half in ((9, 1, slice(0, 2)), (10, -1, slice(2, 4))):
                    got(slot)
                    part = self.view(color, {a: everything, b: half, c: self.p.along(c, 2)})
                    self.go(color, slot + 5, part, part, self.p.other())
            if number == 6:
                got(11, 12, 13, 14, 15)

    def finish(self):
        for copy in self.copies.values():
            copy.wait_send()


def gather_parts(core, ff, d):
    gu = [(slice(None), slice(*cut)) for cut in thirds(ff)]
    half = pl.ds(pl.multiple_of(core * (d // 2), 128), d // 2)
    down = [(slice(*cut), half) for cut in ((32, 40), (0, 16), (16, 32))]
    return gu, down


def gather_kernel(g_ref, u_ref, d_ref, gu_full, d_full, mine, own_sem, send, recv):
    place = Place()
    layers = g_ref.shape[0]
    for n in range(layers):
        mine[n, 0] = g_ref[n]
        mine[n, 1] = u_ref[n]
    enter(place, (1, -1, 2), 1)
    gu_parts, d_parts = gather_parts(place.core, g_ref.shape[-1], d_ref.shape[-1])
    half = d_parts[0][1]
    x, y, z = place.at
    own = []
    for n in range(layers):
        for k, (src, dst) in enumerate(
            (
                (mine.at[n, place.core], gu_full.at[n, place.core, x, y, z]),
                (d_ref.at[n, :, half], d_full.at[n, x, y, z, :, half]),
            )
        ):
            own.append(pltpu.make_async_copy(src, dst, own_sem.at[2 * n + k]))
            own[-1].start()
    jobs = []
    for n in range(layers):
        jobs.append(Gather(place, gu_full.at[n, place.core], mine.at[n, place.core], gu_parts, send.at[2 * n], recv.at[2 * n]))
        jobs.append(Gather(place, d_full.at[n], d_ref.at[n], d_parts, send.at[2 * n + 1], recv.at[2 * n + 1]))
    for t in range(7 + len(jobs) - 1):
        if t == 1:
            for copy in own:
                copy.wait()
        for k, job in enumerate(jobs):
            if 0 <= t - k < 7:
                job.stage(t - k)
    for job in jobs:
        job.finish()


def gather(wg, wu, wd):
    layers, rows, ff = wg.shape
    drows, d = wd.shape[1:]
    return pl.pallas_call(
        gather_kernel,
        out_shape=(
            jax.ShapeDtypeStruct((layers, 2, 4, 4, 4, rows, ff), BF),
            jax.ShapeDtypeStruct((layers, 4, 4, 4, drows, d), BF),
        ),
        in_specs=[VM] * 3,
        out_specs=(ANY, ANY),
        scratch_shapes=[
            pltpu.VMEM((layers, 2, rows, ff), BF),
            pltpu.SemaphoreType.DMA((2 * layers,)),
            pltpu.SemaphoreType.DMA((2 * layers, 3, 16)),
            pltpu.SemaphoreType.DMA((2 * layers, 3, 16)),
        ],
        compiler_params=pltpu.CompilerParams(collective_id=0, has_side_effects=True),
        name="gather",
    )(wg, wu, wd)


class Scatter:
    def __init__(self, place, mine, out, in_a, in_h, acc_b, send_b, in_b, in_bh, acc_c, send_c, in_c, send, recv):
        self.p, self.mine, self.out = place, mine, out
        self.in_a, self.in_h, self.acc_b, self.send_b, self.in_b, self.in_bh = in_a, in_h, acc_b, send_b, in_b, in_bh
        self.acc_c, self.send_c, self.in_c, self.send, self.recv = acc_c, send_c, in_c, send, recv
        self.cuts = thirds(mine.shape[-1])
        self.copies = {}

    def go(self, color, slot, src, dst, axis, step):
        copy = pltpu.make_async_remote_copy(
            src_ref=src, dst_ref=dst, send_sem=self.send.at[color, slot], recv_sem=self.recv.at[color, slot], device_id=self.p.peer(axis, step),
            device_id_type=MESH,
        )
        copy.start()
        self.copies[color, slot] = copy

    def stage(self, number):
        for color, (a, b, c) in enumerate(SCATTER_ORDERS):
            cut = slice(*self.cuts[color])
            got = lambda *slots: [self.copies[color, s].wait_recv() for s in slots]

            def block(where, i, j):
                at = [None] * 3
                at[a], at[b], at[c] = self.p.along(a, where), i, j
                return (*at, slice(None), cut)

            if number == 0:
                for slot, step in ((0, 1), (1, -1)):
                    at = [slice(None)] * 3
                    at[a], at[b] = self.p.along(a, 2), pl.ds(2 * slot, 2)
                    self.go(color, slot, self.mine.at[(*at, slice(None), cut)], self.in_h[color].at[slot], a, step)
            if number == 1:
                for slot, step in ((0, 1), (1, -1)):
                    got(slot)

                    @pl.loop(0, 8)
                    def _(k):
                        i, j = k // 4, k % 4
                        at = block(step, 2 * slot + i, j)
                        self.mine[at] = (self.mine[at].astype(F32) + self.half(color, a, b, c, slot, i, j)).astype(BF)

                for slot, step in ((0, 1), (1, -1)):
                    at = [slice(None)] * 3
                    at[a] = self.p.along(a, step)
                    self.go(color, 2 + slot, self.mine.at[(*at, slice(None), cut)], self.in_a[color].at[slot], a, step)
            if number == 2:
                got(2, 3)

                @pl.loop(0, 16)
                def _(k):
                    i, j = k // 4, k % 4
                    l, m = (i, j) if b < c else (j, i)
                    term = self.mine[block(0, i, j)].astype(F32)
                    total = term + self.in_a[color][0, l, m].astype(F32) + self.in_a[color][1, l, m].astype(F32)
                    self.acc_b[color][i, j] = total
                    self.send_b[color][i, j] = total.astype(BF)

                for slot, step in ((0, 1), (1, -1)):
                    src = self.send_b[color].at[self.p.along(b, 2), pl.ds(2 * slot, 2)]
                    self.go(color, 4 + slot, src, self.in_bh[color].at[slot], b, step)
            if number == 3:
                for slot, step in ((0, 1), (1, -1)):
                    got(4 + slot)
                    i = self.p.along(b, step)

                    @pl.loop(0, 2)
                    def _(j):
                        total = self.acc_b[color][i, 2 * slot + j] + self.in_bh[color][slot, j].astype(F32)
                        self.send_b[color][i, 2 * slot + j] = total.astype(BF)

                for slot, step in ((0, 1), (1, -1)):
                    self.go(color, 6 + slot, self.send_b[color].at[self.p.along(b, step)], self.in_b[color].at[slot], b, step)
            if number == 4:
                got(6, 7)

                @pl.loop(0, 4)
                def _(j):
                    total = self.acc_b[color][self.p.at[b], j] + self.in_b[color][0, j].astype(F32) + self.in_b[color][1, j].astype(F32)
                    self.acc_c[color][j] = total
                    self.send_c[color][j] = total.astype(BF)

                for slot, step in enumerate((1, -1, 2)):
                    self.go(color, 8 + slot, self.send_c[color].at[self.p.along(c, step)], self.in_c[color].at[slot], c, step)
            if number == 5:
                got(8, 9, 10)
                total = self.acc_c[color][self.p.at[c]]
                for slot in range(3):
                    total = total + self.in_c[color][slot].astype(F32)
                self.out[:, cut] = total.astype(BF)

    def half(self, color, a, b, c, slot, i, j):
        l, m = (i, j) if b < c else (j, i)
        return self.in_h[color][slot, l, m].astype(F32)

    def finish(self):
        for copy in self.copies.values():
            copy.wait_send()


SCATTER_STAGES = 6


def scatter_scratch(rows, columns):
    shapes = {k: [] for k in ("in_a", "in_h", "acc_b", "send_b", "in_b", "in_bh", "acc_c", "send_c", "in_c")}
    for (lo, hi), (a, b, c) in zip(thirds(columns), SCATTER_ORDERS):
        w = hi - lo
        half = (2, 4) if b < c else (4, 2)
        for name, shape, kind in (
            ("in_a", (2, 4, 4), BF), ("in_h", (2, *half), BF), ("acc_b", (4, 4), F32), ("send_b", (4, 4), BF), ("in_b", (2, 4), BF),
            ("in_bh", (2, 2), BF), ("acc_c", (4,), F32), ("send_c", (4,), BF), ("in_c", (3,), BF),
        ):
            shapes[name].append(pltpu.VMEM((*shape, rows, w), kind))
    return list(shapes.values())


def scatter_kernel(n, *refs):
    terms, outs = refs[:n], refs[n : 2 * n]
    mine, scratch, load, send, recv = refs[2 * n : 3 * n], refs[3 * n : 4 * n], *refs[4 * n :]
    place = Place()
    loads = [pltpu.make_async_copy(terms[k], mine[k], load.at[k]) for k in range(n)]
    for copy in loads:
        copy.start()
    enter(place, (1, -1, 2), 0)
    jobs = [Scatter(place, mine[k], outs[k], *scratch[k], send.at[k], recv.at[k]) for k in range(n)]
    skew = 2
    for t in range(SCATTER_STAGES + skew * (n - 1)):
        for k, job in enumerate(jobs):
            if t - skew * k == 0:
                loads[k].wait()
            if 0 <= t - skew * k < SCATTER_STAGES:
                job.stage(t - skew * k)
    for job in jobs:
        job.finish()


def scatter(terms, number):
    n = len(terms)
    return pl.pallas_call(
        functools.partial(scatter_kernel, n),
        out_shape=tuple(jax.ShapeDtypeStruct(t.shape[3:], BF) for t in terms),
        in_specs=[ANY] * n,
        out_specs=(VM,) * n,
        scratch_shapes=[
            *(pltpu.VMEM(t.shape, BF) for t in terms),
            *(scatter_scratch(*t.shape[3:]) for t in terms),
            pltpu.SemaphoreType.DMA((n,)),
            pltpu.SemaphoreType.DMA((n, 3, 11)),
            pltpu.SemaphoreType.DMA((n, 3, 11)),
        ],
        compiler_params=pltpu.CompilerParams(collective_id=number, has_side_effects=True, vmem_limit_bytes=60 * 2**20),
        name=f"scatter{number}",
    )(*terms)


def matmul(a, w):
    return jnp.dot(a, w, preferred_element_type=F32).astype(BF)


def normed(h):
    wide = h.astype(F32)
    scale = lax.rsqrt(jnp.mean(wide**2, -1, keepdims=True) + 1e-6)
    return (wide * scale).astype(BF)


def layer(h, w):
    a = normed(h)
    gate = jnp.dot(a, w["w_gate"], preferred_element_type=F32)
    up = jnp.dot(a, w["w_up"], preferred_element_type=F32)
    return h + matmul((jax.nn.silu(gate) * up).astype(BF), w["w_down"])


def stack(weights, h):
    for w in weights:
        h = layer(h, w)
    return h


def solution(mesh):
    def step(x, dy, wg, wu, wd):
        layers, rows, ff = wg.shape
        drows, d = wd.shape[1:]
        gu, down = gather(wg, wu, wd)
        gu = gu.reshape(layers, 2, d, ff)
        down = down.reshape(layers, ff, d)
        weights = [{"w_gate": gu[n, 0], "w_up": gu[n, 1], "w_down": down[n]} for n in range(layers)]
        _, back = jax.vjp(stack, weights, x[0])
        by_weights, by_x = back(dy[0])
        outs = {name: [] for name in NAMES}
        for n in range(layers):
            shaped = [t.reshape(4, 4, 4, t.shape[0] // 64, t.shape[1]) for t in (by_weights[n][name] for name in NAMES)]
            for name, out in zip(NAMES, scatter(shaped, 1 + n)):
                outs[name].append(out)
        return (by_x[None], *(jnp.stack(outs[name]) for name in NAMES))

    seq, rows = P(("rep", "dp"), None, None), P(None, "dp", None)
    return jax.shard_map(
        step, mesh=mesh, in_specs=(seq, seq, rows, rows, rows), out_specs=(seq, *(P("rep", "dp", None),) * 3), check_vma=False
    )
```

time: 2690 us -> 645 us (0.24)
  waiting for transfers between devices: 2240 us -> 0 us
  Pallas kernels: 0 us -> 244 us
  other arithmetic: 78.4 us -> 17.2 us
  matrix products: 313 us -> 343 us
    unnamed x18 -> x0, waiting for transfers between devices: 1960 us -> none
    squeeze x6 -> x0, waiting for transfers between devices: 277 us -> none  [stack(): h = layer(h, {name: w[number] for name, w in weights.items()})]
    pallas_call x0 -> x3, Pallas kernels: none -> 244 us  [the longest x2 164 us: scatter(): pl.pallas_call(functools.partial(scatter_kernel, n), out_shape=tuple((jax...]
    unnamed x3 -> x1, other arithmetic: 55.8 us -> 0.01 us
    dot_general x17, matrix products: 313 us -> 343 us  [the longest x6 125 us: layer(): up = jnp.dot(a, w['w_up'], preferred_element_type=F32)]
  transfers between devices with their start and end apart: 12 -> 0, of which waited for: 12 -> 0; matrix products, arithmetic and copies ran while one was open for 15% -> 0% of each run, Pallas kernels for 0% -> 0%
where the time goes in v1:
time: 645 us; the launch traced here: 636 us
  matrix products  343 us (53%)
  Pallas kernels  244 us (38%)
  local copies, waits for them, and re-layouts  30.1 us (5%)
  other arithmetic  17.2 us (3%)
    pallas_call x2, Pallas kernels, scatter(): pl.pallas_call(functools.partial(scatter_kernel, n), out_shape=tuple((jax...  164 us
    dot_general x6, matrix products, layer(): up = jnp.dot(a, w['w_up'], preferred_element_type=F32)  125 us
    dot_general x6, matrix products, layer(): gate = jnp.dot(a, w['w_gate'], preferred_element_type=F32)  117 us
    dot_general x5, matrix products, matmul(): return jnp.dot(a, w, preferred_element_type=F32).astype(BF)  101 us
    pallas_call x1, Pallas kernels, gather(): pl.pallas_call(gather_kernel, out_shape=(jax.ShapeDtypeStruct((layers, 2,...  80.7 us
    unnamed x37, local copies, waits for them, and re-layouts  20 us

profile of v1, /device:TPU:0, one launch (start us, length us, event | category | flops | bytes accessed | tf_op | source)
XLA Modules:
  0.0 636.5 jit_solution(16183416405416794928)
XLA Ops:
  0.6 6.4 %copy.10 = bf16[1,2048,1024]{1,2,0:T(8,128)(2,1)} copy(bf16[1,2048,1024]{2,1,0:T(8,128)(2,1)} %param.5) | data formatting | bytes 8388608 | tf_op args[0]
  7.1 3.1 fusion.15
  10.1 0.6 copy-done.9
  10.7 6.6 %copy.9 = bf16[1,2048,1024]{1,2,0:T(8,128)(2,1)} copy(bf16[1,2048,1024]{2,1,0:T(8,128)(2,1)} %param.6) | data formatting | bytes 8388608 | tf_op args[1]
  17.3 80.7 %gather.1 = (bf16[2,2,4,4,4,16,2560]{6,5,4,3,2,1,0:T(8,128)(2,1)}, bf16[2,4,4,4,40,1024]{5,4,3,2,1,0:T(8,128)(2,1)}) custom-call(bf16[2,16,2560]{2,1,0:T(8,128)(2,1)} %g_ref.1, bf16[2,16,2560]{2,1,0:T(8,128)(2,1)} %u_ref.1, bf16[2,40,1024]{2,1,0:T(8,128)(2,1)} %d_ref.1), custom_call_target="tpu_custom_call" | custom-call | tf_op jit(solution)/shard_map/gather/pallas_call | solution.py:153
  98.0 10.1 %fusion.51 = (bf16[1,4,4,4,40,1024]{5,4,3,2,1,0:T(8,128)(2,1)}, bf16[1,4,4,4,40,1024]{5,4,3,2,1,0:T(8,128)(2,1)}) fusion(bf16[2,4,4,4,40,1024]{5,4,3,2,1,0:T(8,128)(2,1)} %get-tuple-element.13), kind=kLoop, calls=%fused_computation.78 | loop fusion | bytes 20971520 | tf_op jit(solution)/shard_map/slice | solution.py:356
  108.1 16.9 %convolution_convert_fusion.1 = bf16[2560,2048]{0,1:T(8,128)(2,1)} fusion(bf16[2560,1024]{1,0:T(8,128)(2,1)} %bitcast.91, bf16[1,2048,1024]{2,1,0:T(8,128)(2,1)} %param.6), kind=kOutput, calls=%fused_computation.29 | convolution fusion | flops 10742661120 | bytes 19922944 | tf_op jit(solution)/shard_map/transpose(jvp())/dot_general | solution.py:327
  125.0 17.4 %fusion.25 = f32[2048,2560]{1,0:T(8,128)} fusion(bf16[2,2,1024,2560]{3,2,1,0:T(8,128)(2,1)} %bitcast.104, bf16[1,2048,1024]{2,1,0:T(8,128)(2,1)S(1)} %copy-done.5, f32[2048]{0:T(1024)S(1)} %fusion.44), kind=kOutput, calls=%fused_computation.55 | convolution fusion | flops 10743709696 | bytes 30416896 | tf_op jit(solution)/shard_map/jvp()/dot_general | solution.py:338
  142.4 26.7 %multiply_convert_fusion.1 = (bf16[2048,2560]{1,0:T(8,128)(2,1)}, f32[2048,2560]{1,0:T(8,128)}) fusion(f32[2048,2560]{1,0:T(8,128)} %fusion.25, bf16[2,2,1024,2560]{3,2,1,0:T(8,128)(2,1)} %bitcast.105, bf16[1,2048,1024]{2,1,0:T(8,128)(2,1)} %param.5, f32[2048]{0:T(1024)S(1)} %fusion.44), kind=kOutput, calls=%fused_computation.13 | convolution fusion | flops 10775166976 | bytes 61874176 | tf_op jit(solution)/shard_map/jvp()/dot_general | solution.py:339
  169.0 17.8 %fusion.18 = (f32[2048]{0:T(1024)S(1)}, bf16[2048,1024]{0,1:T(8,128)(2,1)}) fusion(bf16[2048,2560]{1,0:T(8,128)(2,1)} %get-tuple-element.26, bf16[2560,1024]{1,0:T(8,128)(2,1)} %bitcast.87, bf16[1,2048,1024]{1,2,0:T(8,128)(2,1)S(1)} %copy-done), kind=kOutput, calls=%fused_computation.40 | convolution fusion | flops 10747901952 | bytes 24125440 | tf_op jit(solution)/shard_map/jvp()/dot_general | solution.py:327
  186.9 18.3 %fusion.29 = f32[2048,2560]{1,0:T(8,128)} fusion(bf16[2,2,1024,2560]{3,2,1,0:T(8,128)(2,1)} %bitcast.106, bf16[2048,1024]{0,1:T(8,128)(2,1)} %get-tuple-element.29, f32[2048]{0:T(1024)S(1)} %fusion.45), kind=kOutput, calls=%fused_computation.59 | convolution fusion | flops 10743709696 | bytes 30416896 | tf_op jit(solution)/shard_map/jvp()/dot_general | solution.py:339
  205.2 32.1 %fusion.1 = (bf16[2048,2560]{1,0:T(8,128)(2,1)}, f32[2048,2560]{1,0:T(8,128)}) fusion(f32[2048,2560]{1,0:T(8,128)} %fusion.29, bf16[2560,2048]{0,1:T(8,128)(2,1)} %convolution_convert_fusion.1, bf16[2,2,1024,2560]{3,2,1,0:T(8,128)(2,1)} %bitcast.107, bf16[2048,1024]{0,1:T(8,128)(2,1)} %get-tuple-element.29, f32[2048]{0:T(1024)S(1)} %fusion.45), kind=kOutput, calls=%fused_computation.5 | convolution fusion | flops 10806624256 | bytes 72359936 | tf_op jit(solution)/shard_map/jvp()/dot_general | solution.py:338
  237.4 22.1 %fusion.21 = bf16[2560,1024]{1,0:T(8,128)(2,1)} fusion(f32[2048,2560]{1,0:T(8,128)} %fusion.29, bf16[1,2048,1024]{2,1,0:T(8,128)(2,1)} %param.6, f32[2048,2560]{1,0:T(8,128)} %get-tuple-element.31), kind=kOutput, calls=%fused_computation.44 | convolution fusion | flops 10771496960 | bytes 51380224 | tf_op jit(solution)/shard_map/transpose(jvp())/dot_general | solution.py:327
  259.5 19.8 %fusion.7 = bf16[2048,1024]{0,1:T(8,128)(2,1)} fusion(bf16[2560,2048]{0,1:T(8,128)(2,1)} %convolution_convert_fusion.1, bf16[2,2,1024,2560]{3,2,1,0:T(8,128)(2,1)} %bitcast.108, f32[2048,2560]{1,0:T(8,128)} %get-tuple-element.31), kind=kOutput, calls=%fused_computation.25 | convolution fusion | flops 10768875520 | bytes 40894464 | tf_op jit(solution)/shard_map/transpose(jvp())/dot_general | solution.py:339
  279.3 20.4 %fusion.23 = bf16[1024,2560]{1,0:T(8,128)(2,1)} fusion(bf16[2560,2048]{0,1:T(8,128)(2,1)} %convolution_convert_fusion.1, bf16[2048,1024]{0,1:T(8,128)(2,1)} %get-tuple-element.29, f32[2048]{0:T(1024)S(1)} %fusion.45, f32[2048,2560]{1,0:T(8,128)} %get-tuple-element.31), kind=kOutput, calls=%fused_computation.46 | convolution fusion | flops 10777788416 | bytes 40902656 | tf_op jit(solution)/shard_map/transpose(jvp())/dot_general | solution.py:339
  299.7 18.9 %fusion.20 = (f32[2048]{0:T(1024)S(1)}, bf16[2048,1024]{0,1:T(8,128)(2,1)}) fusion(bf16[2048,1024]{0,1:T(8,128)(2,1)} %get-tuple-element.29, bf16[2048,1024]{0,1:T(8,128)(2,1)} %fusion.7, bf16[2048,2560]{1,0:T(8,128)(2,1)} %get-tuple-element.30, bf16[2,2,1024,2560]{3,2,1,0:T(8,128)(2,1)} %bitcast.109), kind=kOutput, calls=%fused_computation.42 | convolution fusion | flops 10747901952 | bytes 28319744 | tf_op jit(solution)/shard_map/transpose(jvp())/dot_general | solution.py:338
  318.5 15.7 %convolution_convert_fusion.2 = bf16[1024,2560]{1,0:T(8,128)(2,1)} fusion(bf16[2048,2560]{1,0:T(8,128)(2,1)} %get-tuple-element.30, bf16[2048,1024]{0,1:T(8,128)(2,1)S(1)} %copy-done.4, f32[2048]{0:T(1024)S(1)} %fusion.45), kind=kOutput, calls=%fused_computation.47 | convolution fusion | flops 10743709696 | bytes 19931136 | tf_op jit(solution)/shard_map/transpose(jvp())/dot_general | solution.py:338
  334.2 83.0 %scatter2.1 = (bf16[16,2560]{1,0:T(8,128)(2,1)}, bf16[16,2560]{1,0:T(8,128)(2,1)}, bf16[40,1024]{1,0:T(8,128)(2,1)}) custom-call(bf16[4,4,4,16,2560]{4,3,2,1,0:T(8,128)(2,1)} %bitcast.97, bf16[4,4,4,16,2560]{4,3,2,1,0:T(8,128)(2,1)} %bitcast.96, bf16[4,4,4,40,1024]{4,3,2,1,0:T(8,128)(2,1)} %bitcast.95), custom_call_target="tpu_custom_call" | custom-call | tf_op jit(solution)/shard_map/scatter2/pallas_call | solution.py:309
  417.3 0.0 slice-start
  417.3 6.4 %fusion.33 = bf16[2048,1024]{0,1:T(8,128)(2,1)S(1)} fusion(bf16[2048,1024]{0,1:T(8,128)(2,1)} %get-tuple-element.29, bf16[2048,1024]{0,1:T(8,128)(2,1)} %get-tuple-element.33, bf16[1,2048,1024]{1,2,0:T(8,128)(2,1)} %copy.9, f32[2048]{0:T(1024)S(1)} %multiply_multiply_fusion.1, f32[2048]{0:T(1024)S(1)} %fusion.45), kind=kLoop, calls=%fused_computation.63 | loop fusion | flops 14680064 | bytes 16793600 | tf_op jit(solution)/shard_map/transpose(jvp())/add_any | solution.py:331
  423.7 17.2 %convolution_convert_fusion.3 = bf16[2560,1024]{1,0:T(8,128)(2,1)} fusion(bf16[2048,2560]{1,0:T(8,128)(2,1)} %get-tuple-element.26, bf16[2048,1024]{0,1:T(8,128)(2,1)S(1)} %fusion.33), kind=kOutput, calls=%fused_computation.48 | convolution fusion | flops 10740039680 | bytes 19922944 | tf_op jit(solution)/shard_map/transpose(jvp())/dot_general | solution.py:327
  440.9 26.8 %fusion.3 = (bf16[2048,2560]{1,0:T(8,128)(2,1)}, bf16[2048,2560]{1,0:T(8,128)(2,1)}) fusion(f32[2048,2560]{1,0:T(8,128)} %fusion.25, f32[2048,2560]{1,0:T(8,128)} %get-tuple-element.27, bf16[2048,1024]{0,1:T(8,128)(2,1)S(1)} %fusion.33, bf16[2560,1024]{1,0:T(8,128)(2,1)S(1)} %bitcast.90), kind=kOutput, calls=%fused_computation.7 | convolution fusion | flops 10805575680 | bytes 72351744 | tf_op jit(solution)/shard_map/transpose(jvp())/dot_general | solution.py:327
  467.7 20.0 %fusion.9 = bf16[2048,1024]{0,1:T(8,128)(2,1)} fusion(bf16[2048,2560]{1,0:T(8,128)(2,1)} %get-tuple-element.35, bf16[2,2,1024,2560]{3,2,1,0:T(8,128)(2,1)} %bitcast.110, f32[2048,2560]{1,0:T(8,128)} %fusion.25), kind=kOutput, calls=%fused_computation.27 | convolution fusion | flops 10768875520 | bytes 40894464 | tf_op jit(solution)/shard_map/transpose(jvp())/dot_general | solution.py:339
  487.7 20.2 %fusion.22 = bf16[1024,2560]{1,0:T(8,128)(2,1)} fusion(bf16[2048,2560]{1,0:T(8,128)(2,1)} %get-tuple-element.35, bf16[1,2048,1024]{1,2,0:T(8,128)(2,1)} %copy.10, f32[2048]{0:T(1024)S(1)} %copy-done.12, f32[2048,2560]{1,0:T(8,128)} %fusion.25), kind=kOutput, calls=%fused_computation.45 | convolution fusion | flops 10777788416 | bytes 40902656 | tf_op jit(solution)/shard_map/transpose(jvp())/dot_general | solution.py:339
  507.9 17.8 %fusion.16 = (f32[2048]{0:T(1024)S(1)}, bf16[2048,1024]{0,1:T(8,128)(2,1)S(1)}) fusion(bf16[1,2048,1024]{1,2,0:T(8,128)(2,1)} %copy.10, bf16[2048,1024]{0,1:T(8,128)(2,1)} %fusion.9, bf16[2048,2560]{1,0:T(8,128)(2,1)} %get-tuple-element.34, bf16[2,2,1024,2560]{3,2,1,0:T(8,128)(2,1)} %bitcast.111), kind=kOutput, calls=%fused_computation.38 | convolution fusion | flops 10747901952 | bytes 28319744 | tf_op jit(solution)/shard_map/transpose(jvp())/dot_general | solution.py:338
  525.7 0.0 copy-start.10
  525.7 15.4 %convolution_convert_fusion.4 = bf16[1024,2560]{1,0:T(8,128)(2,1)} fusion(bf16[2048,2560]{1,0:T(8,128)(2,1)} %get-tuple-element.34, bf16[1,2048,1024]{1,2,0:T(8,128)(2,1)S(1)} %copy-done.1, f32[2048]{0:T(1024)S(1)} %copy-done.12), kind=kOutput, calls=%fused_computation.49 | convolution fusion | flops 10743709696 | bytes 19931136 | tf_op jit(solution)/shard_map/transpose(jvp())/dot_general | solution.py:338
  541.2 4.5 fusion.32
  545.7 6.4 %copy.12 = bf16[1,2048,1024]{2,1,0:T(8,128)(2,1)} copy(bf16[1,2048,1024]{1,2,0:T(8,128)(2,1)} %fusion.32) | data formatting | bytes 8388608
  552.1 80.7 %scatter1.1 = (bf16[16,2560]{1,0:T(8,128)(2,1)}, bf16[16,2560]{1,0:T(8,128)(2,1)}, bf16[40,1024]{1,0:T(8,128)(2,1)}) custom-call(bf16[4,4,4,16,2560]{4,3,2,1,0:T(8,128)(2,1)} %bitcast.94, bf16[4,4,4,16,2560]{4,3,2,1,0:T(8,128)(2,1)} %bitcast.93, bf16[4,4,4,40,1024]{4,3,2,1,0:T(8,128)(2,1)} %bitcast.92), custom_call_target="tpu_custom_call" | custom-call | tf_op jit(solution)/shard_map/scatter1/pallas_call | solution.py:309
  632.8 1.7 pad_maximum_fusion
  634.5 1.6 pad_maximum_fusion.2
  (36 shorter events, 0.1 us)
Async XLA Ops:
  10.1 0.6 copy-start.9
  10.7 131.6 %copy-start.11 = (f32[2048]{0:T(1024)}, f32[2048]{0:T(1024)S(1)}, u32[]{:S(2)}) copy-start(f32[2048]{0:T(1024)S(1)} %fusion.44) | copy-start | bytes 24580
  108.1 16.9 %copy-start.5 = (bf16[1,2048,1024]{2,1,0:T(8,128)(2,1)S(1)}, bf16[1,2048,1024]{2,1,0:T(8,128)(2,1)}, u32[]{:S(2)}) copy-start(bf16[1,2048,1024]{2,1,0:T(8,128)(2,1)} %param.5) | copy-start | bytes 12582916
  142.4 26.7 %copy-start = (bf16[1,2048,1024]{1,2,0:T(8,128)(2,1)S(1)}, bf16[1,2048,1024]{1,2,0:T(8,128)(2,1)}, u32[]{:S(2)}) copy-start(bf16[1,2048,1024]{1,2,0:T(8,128)(2,1)} %copy.10) | copy-start | bytes 12582916
  186.9 18.4 %copy-start.13 = (f32[2048]{0:T(1024)}, f32[2048]{0:T(1024)S(1)}, u32[]{:S(2)}) copy-start(f32[2048]{0:T(1024)S(1)} %get-tuple-element.28) | copy-start | bytes 24580
  299.7 18.9 %copy-start.4 = (bf16[2048,1024]{0,1:T(8,128)(2,1)S(1)}, bf16[2048,1024]{0,1:T(8,128)(2,1)}, u32[]{:S(2)}) copy-start(bf16[2048,1024]{0,1:T(8,128)(2,1)} %get-tuple-element.29) | copy-start | bytes 12582916
  334.2 83.1 %copy-start.14 = (f32[2048]{0:T(1024)S(1)}, f32[2048]{0:T(1024)}, u32[]{:S(2)}) copy-start(f32[2048]{0:T(1024)} %copy-done.13) | copy-start | bytes 24580
  417.3 23.7 %slice-start = ((s8[5242880]{0:T(1024)(128)(4,1)}), s8[4194304]{0:T(1024)(128)(4,1)S(1)}, s32[]{:S(2)}) async-start(s8[5242880]{0:T(1024)(128)(4,1)} %bitcast.88), calls=%async_computation | async-start | bytes 8388608
  423.7 17.3 %copy-start.2 = (bf16[2048,1024]{0,1:T(8,128)(2,1)}, bf16[2048,1024]{0,1:T(8,128)(2,1)S(1)}, u32[]{:S(2)}) copy-start(bf16[2048,1024]{0,1:T(8,128)(2,1)S(1)} %fusion.33) | copy-start | bytes 12582916
  423.7 17.3 %slice-start.1 = ((s8[5242880]{0:T(1024)(128)(4,1)}), s8[1048576]{0:T(1024)(128)(4,1)S(1)}, s32[]{:S(2)}) async-start(s8[5242880]{0:T(1024)(128)(4,1)} %bitcast.88), calls=%async_computation.1 | async-start | bytes 2097152
  467.7 20.0 %copy-start.12 = (f32[2048]{0:T(1024)S(1)}, f32[2048]{0:T(1024)}, u32[]{:S(2)}) copy-start(f32[2048]{0:T(1024)} %copy-done.11) | copy-start | bytes 24580
  507.9 17.8 %copy-start.1 = (bf16[1,2048,1024]{1,2,0:T(8,128)(2,1)S(1)}, bf16[1,2048,1024]{1,2,0:T(8,128)(2,1)}, u32[]{:S(2)}) copy-start(bf16[1,2048,1024]{1,2,0:T(8,128)(2,1)} %copy.10) | copy-start | bytes 12582916
  525.7 15.5 %copy-start.10 = (f32[2048]{0:T(1024)S(1)}, f32[2048]{0:T(1024)}, u32[]{:S(2)}) copy-start(f32[2048]{0:T(1024)} %copy-done.9) | copy-start | bytes 24580
  525.7 15.5 %copy-start.3 = (bf16[2048,1024]{0,1:T(8,128)(2,1)S(1)}, bf16[2048,1024]{0,1:T(8,128)(2,1)}, u32[]{:S(2)}) copy-start(bf16[2048,1024]{0,1:T(8,128)(2,1)} %copy-done.2) | copy-start | bytes 12582916
  552.1 80.7 %copy-start.7 = (bf16[16,2560]{1,0:T(8,128)(2,1)S(1)}, bf16[16,2560]{1,0:T(8,128)(2,1)}, u32[]{:S(2)}) copy-start(bf16[16,2560]{1,0:T(8,128)(2,1)} %get-tuple-element.15) | copy-start | bytes 245764
  552.1 80.7 %copy-start.8 = (bf16[16,2560]{1,0:T(8,128)(2,1)S(1)}, bf16[16,2560]{1,0:T(8,128)(2,1)}, u32[]{:S(2)}) copy-start(bf16[16,2560]{1,0:T(8,128)(2,1)} %get-tuple-element.17) | copy-start | bytes 245764
  552.1 82.4 %copy-start.6 = (bf16[40,1024]{1,0:T(8,128)(2,1)S(1)}, bf16[40,1024]{1,0:T(8,128)(2,1)}, u32[]{:S(2)}) copy-start(bf16[40,1024]{1,0:T(8,128)(2,1)} %get-tuple-element.19) | copy-start | bytes 245764

commit v2 on v0

v2 whole, which is shorter than its diff:
```python
import jax
import jax.numpy as jnp
from jax import lax
from jax.experimental import pallas as pl
from jax.experimental.pallas import tpu as pltpu
from jax.sharding import PartitionSpec as P

MESH = pl.DeviceIdType.MESH
BF, F32 = jnp.bfloat16, jnp.float32
ANY = pl.BlockSpec(memory_space=pl.ANY)
VM = pl.BlockSpec(memory_space=pltpu.VMEM)
T, D, FF = 2048, 1024, 2560
RING, LANES, ROWS, MXU = 4, 128, 8, 256
CUBE = (RING,) * 3
TILES = 40
AXES = range(3)
STEPS = (1, -1, 2)
SIDES = ((0, 1), (1, -1))
EVERY = slice(None)
VMEM = 63 * 2**20

GATHER_ORDERS = ((2, 1, 0), (0, 2, 1), (1, 0, 2))
SCATTER_ORDERS = ((0, 1, 2), (1, 2, 0), (2, 0, 1))
SHARES = ((0, 14), (14, 27), (27, 40))


class Place:
    def __init__(self):
        self.core = lax.axis_index("rep")
        me = lax.axis_index("dp")
        self.at = (me // RING**2, (me // RING) % RING, me % RING)
        self.on = {(a, step): (self.at[a] + (step + RING)) % RING for a in AXES for step in STEPS}

    def along(self, axis, step):
        return self.on[axis, step]

    def peer(self, axis, step):
        x, y, z = (self.along(a, step) if a == axis else self.at[a] for a in AXES)
        return {"dp": (x * RING + y) * RING + z}

    def other(self):
        return {"rep": 1 - self.core}


def enter(place, other):
    barrier = pltpu.get_barrier_semaphore()
    for axis in AXES:
        for step in STEPS:
            pl.semaphore_signal(barrier, inc=1, device_id=place.peer(axis, step), device_id_type=MESH)
    if other:
        pl.semaphore_signal(barrier, inc=1, device_id=place.other(), device_id_type=MESH)
    pl.semaphore_wait(barrier, len(STEPS) * len(AXES) + other)


def remote(src, dst, send, recv, device):
    return pltpu.make_async_remote_copy(src_ref=src, dst_ref=dst, send_sem=send, recv_sem=recv, device_id=device, device_id_type=MESH)


def normed(h):
    wide = h.astype(F32)
    scale = lax.rsqrt(jnp.mean(wide**2, -1, keepdims=True) + 1e-6)
    return (wide * scale).astype(BF)


def dot(a, b, over_a=1, over_b=0):
    return lax.dot_general(a, b, (((over_a,), (over_b,)), ((), ())), preferred_element_type=F32)


def at_step(hooks, step):
    for number, hook in hooks.items():
        pl.when(step == number)(hook)


class Gather:
    def __init__(self, place, full, mine, parts, send, recv):
        self.p, self.full, self.mine, self.parts, self.send, self.recv = place, full, mine, parts, send, recv

    STARTS = (0, 3, 5, 7, 10, 14, 16)
    CROSS = (9, 12, 13, 14, 15)

    def view(self, color, where):
        at = [where.get(a, self.p.at[a]) for a in AXES]
        return self.full.at[(*at, *self.parts[color])]

    def copy(self, color, slot):
        a, b, c = GATHER_ORDERS[color]
        p = self.p
        sems = self.send.at[color, slot], self.recv.at[color, slot]
        stage = sum(slot >= first for first in self.STARTS) - 1
        k = slot - self.STARTS[stage]
        if stage == 0:
            return remote(self.mine.at[self.parts[color]], self.view(color, {}), *sems, p.peer(a, STEPS[k]))
        axis, done, split = (b, {a: EVERY}, a) if stage < 3 else (c, {a: EVERY, b: EVERY}, b)
        side = k % 2
        step, half = STEPS[side], slice(2 * side, 2 * side + 2)
        where = dict(done)
        if stage in (2, 4):
            where[axis] = p.along(axis, -step)
            if slot not in self.CROSS:
                where[split] = half
        if stage == 5:
            where.update({axis: p.along(axis, 2), split: half})
        block = self.view(color, where)
        return remote(block, block, *sems, p.other() if slot in self.CROSS else p.peer(axis, step))

    def stage(self, number):
        last = len(self.STARTS) - 1
        for color in AXES:
            if number == last:
                wait = self.CROSS
            else:
                wait = [k for k in range(self.STARTS[number - 1], self.STARTS[number]) if k not in self.CROSS] if number else ()
            for slot in wait:
                self.copy(color, slot).wait_recv()
            for slot in range(self.STARTS[number], self.STARTS[number + 1]) if number < last else ():
                self.copy(color, slot).start()

    def finish(self):
        for color in AXES:
            for slot in range(self.STARTS[-1]):
                self.copy(color, slot).wait_send()


def thirds(n):
    cuts = [0]
    for left in (3, 2, 1):
        cuts.append(cuts[-1] + -((cuts[-1] - n // LANES) // left))
    return [(lo * LANES, hi * LANES) for lo, hi in zip(cuts, cuts[1:])]


def gather_parts(core):
    gu = [(EVERY, slice(*cut)) for cut in thirds(FF)]
    half = pl.ds(pl.multiple_of(core * (D // 2), D // 2), D // 2)
    down = [(slice(*cut), EVERY, half) for cut in ((4, 5), (0, 2), (2, 4))]
    return gu, down


def slots(*groups):
    def hook():
        for job, stage in groups:
            job.stage(stage)

    return hook


class Scatter:
    def __init__(self, place, mine, out, number, bufs, send, recv):
        self.p, self.mine, self.out, self.number, self.send, self.recv = place, mine, out, number, send, recv
        self.in_a, self.in_h, self.acc_b, self.send_b, self.in_b, self.in_bh, self.acc_c, self.send_c, self.in_c = bufs

    def term(self, color, where):
        at = dict(zip(SCATTER_ORDERS[color], where))
        return (*(at[axis] for axis in AXES), slice(*SHARES[color]))

    STARTS = (0, 2, 4, 6, 8, 11)

    def copy(self, color, slot):
        a, b, c = SCATTER_ORDERS[color]
        p = self.p
        sems = self.send.at[color, slot], self.recv.at[color, slot]
        twin = self.number % 2
        stage = sum(slot >= first for first in self.STARTS) - 1
        k = slot - self.STARTS[stage]
        step, half = STEPS[k], pl.ds(2 * k, 2)
        if stage == 0:
            src, dst, axis = self.mine.at[self.term(color, (p.along(a, 2), half, EVERY))], self.in_h[color].at[k], a
        elif stage == 1:
            src, dst, axis = self.mine.at[self.term(color, (p.along(a, step), EVERY, EVERY))], self.in_a[color].at[k], a
        elif stage == 2:
            src, dst, axis = self.send_b[color].at[twin, p.along(b, 2), half], self.in_bh[color].at[k], b
        elif stage == 3:
            src, dst, axis = self.send_b[color].at[twin, p.along(b, step)], self.in_b[color].at[k], b
        else:
            src, dst, axis = self.send_c[color].at[twin, p.along(c, step)], self.in_c[color].at[self.number, k], c
        return remote(src, dst, *sems, p.peer(axis, step))

    def stage(self, number):
        last = len(self.STARTS) - 1
        for color, axes in enumerate(SCATTER_ORDERS):
            for slot in range(self.STARTS[number - 1], self.STARTS[number]) if number else ():
                self.copy(color, slot).wait_recv()
            self.sum(number, color, *axes)
            for slot in range(self.STARTS[number], self.STARTS[number + 1]) if number < last else ():
                self.copy(color, slot).start()
            for slot in range(self.STARTS[2], self.STARTS[last]) if number == last else ():
                self.copy(color, slot).wait_send()

    def sum(self, number, color, a, b, c):
        p, mine, twin = self.p, self.mine, self.number % 2
        in_a, in_h, acc_b, send_b, in_b, in_bh = (
            t[color] for t in (self.in_a, self.in_h, self.acc_b, self.send_b, self.in_b, self.in_bh)
        )
        acc_c, send_c, in_c = (t[color] for t in (self.acc_c, self.send_c, self.in_c))
        flip = (lambda i, j: (i, j)) if b < c else (lambda i, j: (j, i))
        if number == 1:
            for slot, step in SIDES:

                @pl.loop(0, 2 * RING)
                def _(k):
                    i, j = k // RING, k % RING
                    at = self.term(color, (p.along(a, step), 2 * slot + i, j))
                    mine[at] = (mine[at].astype(F32) + in_h[(slot, *flip(i, j))].astype(F32)).astype(BF)

        if number == 2:

            @pl.loop(0, RING**2)
            def _(k):
                i, j = k // RING, k % RING
                total = mine[self.term(color, (p.at[a], i, j))].astype(F32)
                total = total + in_a[(0, *flip(i, j))].astype(F32) + in_a[(1, *flip(i, j))].astype(F32)
                acc_b[i, j] = total
                send_b[twin, i, j] = total.astype(BF)

        if number == 3:
            for slot, step in SIDES:
                i = p.along(b, step)

                @pl.loop(0, 2)
                def _(j):
                    send_b[twin, i, 2 * slot + j] = (acc_b[i, 2 * slot + j] + in_bh[slot, j].astype(F32)).astype(BF)

        if number == 4:

            @pl.loop(0, RING)
            def _(j):
                total = acc_b[p.at[b], j] + in_b[0, j].astype(F32) + in_b[1, j].astype(F32)
                acc_c[j] = total
                send_c[twin, j] = total.astype(BF)

        if number == 5:
            total = acc_c[p.at[c]]
            for slot in AXES:
                total = total + in_c[self.number, slot].astype(F32)
            lo, hi = SHARES[color]
            high = self.out.shape[0] // ROWS
            for k in range(lo, hi):
                col, row = k // high, k % high
                self.out[pl.ds(ROWS * row, ROWS), pl.ds(LANES * col, LANES)] = total[k - lo].astype(BF)

    def finish(self):
        for color in AXES:
            for slot in range(self.STARTS[2]):
                self.copy(color, slot).wait_send()


def scatter_scratch(jobs):
    two, ring = (2,), (RING,)
    groups = []
    for (lo, hi), (a, b, c) in zip(SHARES, SCATTER_ORDERS):
        half = two + ring if b < c else ring + two
        shapes = (
            (two + ring + ring, BF), (two + half, BF), (ring + ring, F32), (two + ring + ring, BF), (two + ring, BF), (two + two, BF), (ring, F32),
            (two + ring, BF), ((jobs, len(STEPS)), BF),
        )
        groups.append([pltpu.VMEM((*shape, hi - lo, ROWS, LANES), kind) for shape, kind in shapes])
    return zip(*groups)


def store_tiles(val, store, high):
    for k in range(val.shape[1] // LANES):
        store(k, val[:, LANES * k : LANES * (k + 1)].reshape(-1, high, ROWS, LANES).astype(BF))


def part(k, size):
    return pl.ds(pl.multiple_of(k * size, size), size)


def blocks(shape, places, **mode):
    return pl.BlockSpec(shape, lambda *at: tuple(at[places[k]] if k in places else 0 for k in range(len(shape))), **mode)


def silu_parts(gate):
    s = jax.nn.sigmoid(gate)
    silu = gate * s
    return silu, s + silu * (1 - s)


def forward_kernel(
    g_ref, u_ref, d_ref, x_ref, dy_ref, gu_full, d_full, aT0, gate_up, act1, h1, aT1, act2, dgu2, mine, mine_d, a_v, h_v, t_v, dy_v, sem, send, recv
):
    place = Place()
    core = place.core
    layers = g_ref.shape[0]
    for n in range(layers):
        for k, ref in enumerate((g_ref, u_ref)):
            mine[n, k] = ref[n]
        mine_d[n] = d_ref[n]
    sems = [sem.at[k] for k in range(sem.shape[0])]
    load = pltpu.make_async_copy(x_ref, h_v, sems.pop())
    load_dy = pltpu.make_async_copy(dy_ref, dy_v, sems.pop())
    load.start()
    load_dy.start()
    enter(place, 1)
    gu_parts, d_parts = gather_parts(core)
    half = d_parts[0][-1]
    own, jobs = [], []
    for n in range(layers):
        own.append(pltpu.make_async_copy(mine.at[n, core], gu_full.at[(n, core, *place.at)], sems.pop()))
        own.append(pltpu.make_async_copy(mine_d.at[n, :, :, half], d_full.at[(n, *place.at, EVERY, EVERY, half)], sems.pop()))
        for args in ((gu_full.at[n, core], mine.at[n, core], gu_parts), (d_full.at[n], mine_d.at[n], d_parts)):
            jobs.append(Gather(place, *args, send.at[len(jobs)], recv.at[len(jobs)]))
    j0, *later = jobs
    j1, j2, j3 = later
    j0.stage(0)
    for copy in own:
        copy.start()
    load.wait()

    def norm_rows(k):
        rows = part(k, MXU)
        a = normed(h_v[rows])
        a_v[rows] = a
        t_v[:, rows] = a.T

    pl.loop(0, RING)(norm_rows)
    for copy in own:
        copy.wait()
    j0.stage(1)
    pl.loop(RING, 2 * RING)(norm_rows)
    put = pltpu.make_async_copy(t_v, aT0, sems[0])
    put.start()
    for stage in range(2, 7):
        j0.stage(stage)
        if stage > 2:
            for job in later if stage < 6 else ():
                job.stage(stage - 3)

    hooks = {0: slots((j1, 3), (j2, 3)), 3: slots((j1, 4)), 6: slots((j1, 5), (j2, 4), (j3, 3))}
    wide, tall = 512, 1024

    def gate_up_body(w, out_gu, out_act):
        row, step = pl.program_id(1), pl.program_id(0) * (T // tall) + pl.program_id(1)
        at_step(hooks, step)
        a = a_v[part(row, tall)]
        for k in range(wide // MXU):
            cols = slice(MXU * k, MXU * (k + 1))
            gate, up = (dot(a, w[m, :, :, :, :, cols].reshape(D, MXU)) for m in range(2))
            for m, val in enumerate((gate, up)):
                out_gu[m, :, cols] = val
            out_act[:, cols] = (silu_parts(gate)[0] * up).astype(BF)

    pltpu.emit_pipeline(
        gate_up_body,
        grid=(FF // wide, T // tall),
        in_specs=[blocks((2, *CUBE, 16, wide), {5: 0})],
        out_specs=[blocks((2, tall, wide), {1: 1, 2: 0}), blocks((tall, wide), {0: 1, 1: 0})],
    )(gu_full.at[0], gate_up, act1)
    put.wait()
    j1.stage(6)

    hooks_down = {0: slots((j2, 5), (j3, 4)), 2: slots((j2, 6), (j3, 5))}

    def down_body(act, w, out_h):
        step = pl.program_id(0)
        at_step(hooks_down, step)
        for k in range(wide // MXU):
            rows = slice(MXU * k, MXU * (k + 1))
            there = part(step * (wide // MXU) + k, MXU)
            out = dot(act[rows], w[...].reshape(FF, D)).astype(BF)
            h = (h_v[there].astype(F32) + out.astype(F32)).astype(BF)
            out_h[rows] = h
            a = normed(h)
            a_v[there] = a
            t_v[:, there] = a.T

    pltpu.emit_pipeline(
        down_body,
        grid=(T // wide,),
        in_specs=[blocks((wide, FF), {0: 0}), blocks(d_full.shape[1:], {}, pipeline_mode=pl.Buffered(1))],
        out_specs=[blocks((wide, D), {0: 0})],
    )(act1, d_full.at[0], h1)
    put = pltpu.make_async_copy(t_v, aT1, sems[0])
    put.start()
    load_dy.wait()
    j3.stage(6)

    def second_body(w, wd_block, out_act, out_dgu):
        wd = wd_block[...].reshape(FF // 2 // ROWS, ROWS, D)
        rows = part(pl.program_id(1), wide)
        a, dy = a_v[rows], dy_v[rows]
        for k in range(FF // 2 // MXU):
            cols = slice(MXU * k, MXU * (k + 1))
            gate, up = (dot(a, w[m, :, :, :, :, cols].reshape(D, MXU)) for m in range(2))
            by_act = dot(dy, wd[MXU // ROWS * k : MXU // ROWS * (k + 1)].reshape(MXU, D), 1, 1).astype(BF).astype(F32)
            silu, slope = silu_parts(gate)
            out_act[:, cols] = (silu * up).astype(BF)
            for m, val in enumerate((by_act * up * slope, by_act * silu)):
                out_dgu[m, :, cols] = val.astype(BF)

    pltpu.emit_pipeline(
        second_body,
        grid=(2, T // wide),
        in_specs=[blocks((2, *CUBE, 16, FF // 2), {5: 0}), blocks((2, *d_full.shape[2:]), {0: 0})],
        out_specs=[blocks((wide, FF // 2), {0: 1, 1: 0}), blocks((2, wide, FF // 2), {1: 1, 2: 0})],
    )(gu_full.at[1], d_full.at[1], act2, dgu2)
    put.wait()
    for job in jobs:
        job.finish()


def shaped(*shape, kind=BF):
    return jax.ShapeDtypeStruct(shape, kind)


def calls(kernel, number, ins, outs, scratch):
    return pl.pallas_call(
        kernel,
        out_shape=tuple(shape for shape, _ in outs),
        in_specs=ins,
        out_specs=tuple(spec for _, spec in outs),
        scratch_shapes=scratch,
        compiler_params=pltpu.CompilerParams(collective_id=number, has_side_effects=True, vmem_limit_bytes=VMEM),
        name=kernel.__name__,
    )


def forward(wg, wu, wd, x, dy):
    layers, rows = wg.shape[:-1]
    high = TILES * LANES // D
    outs = [
        shaped(layers, 2, *CUBE, rows, FF), shaped(layers, *CUBE, high, ROWS, D), shaped(D, T), shaped(2, T, FF, kind=F32), shaped(T, FF),
        shaped(T, D), shaped(D, T), shaped(T, FF), shaped(2, T, FF),
    ]
    scratch = [shaped(layers, 2, rows, FF), shaped(layers, high, ROWS, D), shaped(T, D), shaped(T, D), shaped(D, T), shaped(T, D)]
    sems = [(7,), (2 * layers, 3, 16), (2 * layers, 3, 16)]
    scratch = [pltpu.VMEM(t.shape, t.dtype) for t in scratch] + [pltpu.SemaphoreType.DMA(t) for t in sems]
    call = calls(forward_kernel, 0, [VM] * 3 + [ANY] * 2, [(t, ANY) for t in outs], scratch)
    return call(wg, wu, wd.reshape(layers, high, ROWS, D), x, dy)


def down_grad(act, by_out, sink, hooks, outs=(), out_specs=()):
    high = TILES * LANES // D

    def body(act_cols, *refs):
        k = pl.program_id(0)
        at_step(hooks, k)

        def store(c, val):
            sink(k, slice(high * c, high * (c + 1)), val.reshape(RING, RING, high, ROWS, LANES), *refs)

        store_tiles(dot(act_cols[...], by_out[...], 0, 0), store, high)

    pltpu.emit_pipeline(body, grid=(RING,), in_specs=[blocks((T, FF // RING), {1: 0})], out_specs=list(out_specs))(act, *outs)


def gate_up_grads(a_t, dgu, mine, hooks):
    high = TILES * LANES // FF
    wide = 512
    each = FF // wide

    def body(cols):
        k = pl.program_id(0)
        at_step(hooks, k)

        def store(c, val):
            tiles = pl.ds((k % each) * (high * wide // LANES) + high * c, high)
            mine[1 + k // each, :, :, :, tiles] = val.reshape(*CUBE, high, ROWS, LANES)

        store_tiles(dot(a_t[...], cols[...]), store, high)

    pltpu.emit_pipeline(body, grid=(2 * each,), in_specs=[pl.BlockSpec((None, T, wide), lambda k: (k // each, 0, k % each))])(dgu)


def state_grad(dgu, w, h, by_out, out, keep, hooks):
    def body(d, h, out):
        k = pl.program_id(0)
        at_step(hooks, k)
        rows = part(k, MXU)
        by_gate, by_up = (dot(d[m], w[m], 1, 1).astype(BF).astype(F32) for m in range(2))
        by_a = (by_gate + by_up).astype(BF).astype(F32)
        wide = h[...].astype(F32)
        scale = lax.rsqrt(jnp.mean(wide**2, -1, keepdims=True) + 1e-6)
        inner = jnp.mean(by_a * wide, -1, keepdims=True)
        by_norm = (by_a * scale - wide * (inner * scale * scale * scale)).astype(BF)
        total = (by_out[rows].astype(F32) + by_norm.astype(F32)).astype(BF)
        out[...] = total
        if keep is not None:
            keep[rows] = total

    rows = blocks((MXU, D), {0: 0})
    pltpu.emit_pipeline(body, grid=(T // MXU,), in_specs=[blocks((2, MXU, FF), {1: 0}), rows], out_specs=[rows])(dgu, h, out)


def scatter_jobs(place, mine, outs, bufs, send, recv):
    groups = [bufs[k : k + len(SHARES)] for k in range(0, len(bufs), len(SHARES))]
    return [Scatter(place, mine.at[k], out, k, groups, send.at[k], recv.at[k]) for k, out in enumerate(outs)]


def at_slot(jobs, t):
    return slots(*((job, t - 2 * k) for k, job in enumerate(jobs) if 0 <= t - 2 * k < len(Scatter.STARTS)))


def rest_of(jobs, first):
    for t in range(first, len(Scatter.STARTS) + 2 * (len(jobs) - 1)):
        at_slot(jobs, t)()
    for job in jobs:
        job.finish()


def second_kernel(act2, dy, aT1, dgu2, w2, h1, act1, dh1, down1, d_out, g_out, u_out, dy_v, t_v, dh_v, w_v, mine, *more):
    *bufs, sem, send, recv = more
    place = Place()
    loads = [pltpu.make_async_copy(*pair, sem.at[k]) for k, pair in enumerate(((dy, dy_v), (aT1, t_v), (w2.at[1], w_v)))]
    for copy in loads:
        copy.start()
    enter(place, 0)
    jobs = scatter_jobs(place, mine, (d_out, g_out, u_out), bufs, send, recv)
    load_dy, load_t, load_w = loads
    load_dy.wait()

    def keep_down(k, tiles, val):
        mine[0, k, :, :, tiles] = val

    down_grad(act2, dy_v, keep_down, {})
    load_t.wait()
    gate_up_grads(t_v, dgu2, mine, {0: at_slot(jobs, 0), 4: at_slot(jobs, 1), 9: at_slot(jobs, 2)})
    load_w.wait()
    state_grad(dgu2, w_v, h1, dy_v, dh1, dh_v, {2: at_slot(jobs, 3), 6: at_slot(jobs, 4)})

    def put_down(k, tiles, val, out):
        out[:, :, tiles] = val

    down_grad(act1, dh_v, put_down, {1: at_slot(jobs, 5)}, [down1], [blocks((None, *down1.shape[1:]), {0: 0})])
    rest_of(jobs, 6)


SUMS = [((TILES * LANES // D * ROWS, D), VM), ((TILES * LANES // FF * ROWS, FF), VM), ((TILES * LANES // FF * ROWS, FF), VM)]


def scatter_scratch_all():
    return [
        pltpu.VMEM((len(SUMS), *CUBE, TILES, ROWS, LANES), BF),
        *(buf for group in scatter_scratch(len(SUMS)) for buf in group),
        pltpu.SemaphoreType.DMA((4,)),
        *[pltpu.SemaphoreType.DMA((len(SUMS), len(SHARES), Scatter.STARTS[-1]))] * 2,
    ]


def backward(kernel, number, outs, vmem, args):
    outs = [(t, ANY) for t in outs] + [(shaped(*shape), spec) for shape, spec in SUMS]
    return calls(kernel, number, [ANY] * len(args), outs, [pltpu.VMEM(t, BF) for t in vmem] + scatter_scratch_all())(*args)


def second(*args):
    outs = [shaped(T, D), shaped(*CUBE, TILES, ROWS, LANES)]
    return backward(second_kernel, 1, outs, [(T, D), (D, T), (T, D), (2, D, FF)], args)


def first_kernel(dh1, gate_up, wd1, aT0, w1, x, down1, dx, dgu1, d_out, g_out, u_out, dh_v, t_v, wd_v, w_v, mine, *more):
    *bufs, sem, send, recv = more
    place = Place()
    pairs = ((down1, mine.at[0]), (dh1, dh_v), (wd1.at[0], wd_v), (aT0, t_v))
    loads = [pltpu.make_async_copy(*pair, sem.at[k]) for k, pair in enumerate(pairs)]
    for copy in loads:
        copy.start()
    enter(place, 0)
    jobs = scatter_jobs(place, mine, (d_out, g_out, u_out), bufs, send, recv)
    for copy in loads:
        copy.wait()
    load_w = pltpu.make_async_copy(w1.at[0], w_v, sem.at[0])
    load_w.start()
    at_slot(jobs, 0)()
    hooks = {10: at_slot(jobs, 1)}
    wide = 512

    def act_body(gu, out):
        col, row = pl.program_id(0), pl.program_id(1)
        at_step(hooks, col * (T // wide) + row)
        by_act = dot(dh_v[part(row, wide)], wd_v[part(col, wide)], 1, 1).astype(BF).astype(F32)
        silu, slope = silu_parts(gu[0])
        for m, val in enumerate((by_act * gu[1] * slope, by_act * silu)):
            out[m] = val.astype(BF)

    block = blocks((2, wide, wide), {1: 1, 2: 0})
    pltpu.emit_pipeline(act_body, grid=(FF // wide, T // wide), in_specs=[block], out_specs=[block])(gate_up, dgu1)
    gate_up_grads(t_v, dgu1, mine, {5: at_slot(jobs, 2), 9: at_slot(jobs, 3)})
    load_w.wait()
    state_grad(dgu1, w_v, x, dh_v, dx, None, {2: at_slot(jobs, 4), 5: at_slot(jobs, 5)})
    rest_of(jobs, 6)


def first(*args):
    return backward(first_kernel, 2, [shaped(T, D), shaped(2, T, FF)], [(T, D), (D, T), (FF, D), (2, D, FF)], args)


def solution(mesh):
    def step(x, dy, wg, wu, wd):
        x, dy = x[0], dy[0]
        gu, down, aT0, gate_up, act1, h1, aT1, act2, dgu2 = forward(wg, wu, wd, x, dy)
        gu, down = gu.reshape(-1, 2, D, FF), down.reshape(-1, FF, D)
        dh1, down1, d2, g2, u2 = second(act2, dy, aT1, dgu2, gu, h1, act1)
        dx, _, d1, g1, u1 = first(dh1, gate_up, down, aT0, gu, x, down1)
        return dx[None], jnp.stack([g1, g2]), jnp.stack([u1, u2]), jnp.stack([d1, d2])

    seq, rows = P(("rep", "dp"), None, None), P(None, "dp", None)
    return jax.shard_map(
        step, mesh=mesh, in_specs=(seq, seq, rows, rows, rows), out_specs=(seq, *[P("rep", "dp", None)] * 3), check_vma=False
    )
```

time: 2690 us -> 387 us (0.14)
  waiting for transfers between devices: 2240 us -> 0 us
  Pallas kernels: 0 us -> 377 us
  matrix products: 313 us -> 0 us
  other arithmetic: 78.4 us -> 3.25 us
  local copies, waits for them, and re-layouts: 35.4 us -> 4.65 us
    unnamed x18 -> x0, waiting for transfers between devices: 1960 us -> none
    pallas_call x0 -> x3, Pallas kernels: none -> 377 us  [the longest x2 233 us: backward(): calls(kernel, number, [ANY] * len(args), outs, [pltpu.VMEM(t, BF) for t i...]
    dot_general x17 -> x0, matrix products: 313 us -> none  [the longest x6 119 us: layer(): up = jnp.dot(a, w['w_up'], preferred_element_type=jnp.float32)]
    squeeze x6 -> x0, waiting for transfers between devices: 277 us -> none  [stack(): h = layer(h, {name: w[number] for name, w in weights.items()})]
    unnamed x3 -> x0, other arithmetic: 55.8 us -> none
  transfers between devices with their start and end apart: 12 -> 0, of which waited for: 12 -> 0; matrix products, arithmetic and copies ran while one was open for 15% -> 0% of each run, Pallas kernels for 0% -> 0%
where the time goes in v2:
time: 387 us; the launch traced here: 386 us
  Pallas kernels  377 us (97%)
  local copies, waits for them, and re-layouts  4.65 us (1%)
    pallas_call x2, Pallas kernels, backward(): calls(kernel, number, [ANY] * len(args), outs, [pltpu.VMEM(t, BF) for t i...  233 us
    pallas_call x1, Pallas kernels, forward(): return call(wg, wu, wd.reshape(layers, high, ROWS, D), x, dy)  144 us

profile of v2, /device:TPU:0, one launch (start us, length us, event | category | flops | bytes accessed | tf_op | source)
XLA Modules:
  0.0 385.9 jit_solution(11313431169653360346)
XLA Ops:
  0.6 144.4 %forward_kernel.1 = (bf16[2,2,4,4,4,16,2560]{6,5,4,3,2,1,0:T(8,128)(2,1)}, bf16[2,4,4,4,5,8,1024]{6,5,4,3,2,1,0:T(8,128)(2,1)}, bf16[1024,2048]{1,0:T(8,128)(2,1...) custom-call(bf16[2,16,2560]{2,1,0:T(8,128)(2,1)} %g_ref.1, ...), custom_call_target="tpu_custom_call" | custom-call | tf_op jit(solution)/shard_map/forward_kernel/pallas_call | solution.py:428
  145.0 114.1 %second_kernel.1 = (bf16[2048,1024]{1,0:T(8,128)(2,1)}, bf16[4,4,4,40,8,128]{5,4,3,2,1,0:T(8,128)(2,1)}, bf16[40,1024]{1,0:T(8,128)(2,1)}, bf16[16,2560]{1,0:T(8,128)(2,1)}, bf16[16,2560]{1,0:T(8,128)(2,1)}) custom-call(bf16[2048,2560]{1,0:T(8,128)(2,1)} %get-tuple-element.22.act2, bf16[2048,1024]{1,0:T(8,128)(2,1)} %bitcast.15, ...), custom_call_target="tpu_custom_call" | custom-call | tf_op jit(solution)/shard_map/second_kernel/pallas_call | solution.py:541
  259.2 0.0 copy-start.1
  259.2 0.0 copy-start.2
  259.2 0.0 copy-start
  259.2 118.8 %first_kernel.1 = (bf16[2048,1024]{1,0:T(8,128)(2,1)}, bf16[2,2048,2560]{2,1,0:T(8,128)(2,1)}, bf16[40,1024]{1,0:T(8,128)(2,1)}, bf16[16,2560]{1,0:T(8,128)(2,1)}, bf16[16,2560]{1,0:T(8,128)(2,1)}) custom-call(bf16[2048,1024]{1,0:T(8,128)(2,1)} %get-tuple-element.28.dh1, f32[2,2048,2560]{2,1,0:T(8,128)} %get-tuple-element.29.gate_up, ...), custom_call_target="tpu_custom_call" | custom-call | tf_op jit(solution)/shard_map/first_kernel/pallas_call | solution.py:541
  378.0 0.0 copy-done.1
  378.0 0.0 copy-done.2
  378.0 1.7 pad_maximum_fusion
  379.7 0.0 copy-done
  379.7 1.6 pad_maximum_fusion.2
  381.3 4.6 %copy.10 = bf16[1,2048,1024]{2,1,0:T(8,128)(2,1)} copy(bf16[1,2048,1024]{2,1,0:T(8,128)(2,1)} %bitcast.19) | data formatting | bytes 8388608
Async XLA Ops:
  259.2 118.8 %copy-start.1 = (bf16[16,2560]{1,0:T(8,128)(2,1)S(1)}, bf16[16,2560]{1,0:T(8,128)(2,1)}, u32[]{:S(2)}) copy-start(bf16[16,2560]{1,0:T(8,128)(2,1)} %get-tuple-element.35) | copy-start | bytes 245764
  259.2 118.8 %copy-start.2 = (bf16[16,2560]{1,0:T(8,128)(2,1)S(1)}, bf16[16,2560]{1,0:T(8,128)(2,1)}, u32[]{:S(2)}) copy-start(bf16[16,2560]{1,0:T(8,128)(2,1)} %get-tuple-element.37) | copy-start | bytes 245764
  259.2 120.5 %copy-start = (bf16[40,1024]{1,0:T(8,128)(2,1)S(1)}, bf16[40,1024]{1,0:T(8,128)(2,1)}, u32[]{:S(2)}) copy-start(bf16[40,1024]{1,0:T(8,128)(2,1)} %get-tuple-element.39) | copy-start | bytes 245764

commit v3 on v2

--- a/solution.py
+++ b/solution.py
@@ -11,8 +11,10 @@
 VM = pl.BlockSpec(memory_space=pltpu.VMEM)
 T, D, FF = 2048, 1024, 2560
 RING, LANES, ROWS, MXU = 4, 128, 8, 256
+PAIR = 2 * ROWS
 CUBE = (RING,) * 3
-TILES = 40
+UNITS = 20
+HIGH = UNITS * PAIR * LANES // D // ROWS
 AXES = range(3)
 STEPS = (1, -1, 2)
 SIDES = ((0, 1), (1, -1))
@@ -21,7 +23,7 @@
 
 GATHER_ORDERS = ((2, 1, 0), (0, 2, 1), (1, 0, 2))
 SCATTER_ORDERS = ((0, 1, 2), (1, 2, 0), (2, 0, 1))
-SHARES = ((0, 14), (14, 27), (27, 40))
+SHARES = ((0, 7), (7, 14), (14, 20))
 
 
 class Place:
@@ -144,15 +146,15 @@
 
 
 class Scatter:
-    def __init__(self, place, mine, out, number, bufs, send, recv):
-        self.p, self.mine, self.out, self.number, self.send, self.recv = place, mine, out, number, send, recv
+    STARTS = (0, 2, 4, 6, 8, 11)
+
+    def __init__(self, place, mine, put, number, bufs, send, recv):
+        self.p, self.mine, self.put, self.number, self.send, self.recv = place, mine, put, number, send, recv
         self.in_a, self.in_h, self.acc_b, self.send_b, self.in_b, self.in_bh, self.acc_c, self.send_c, self.in_c = bufs
 
     def term(self, color, where):
         at = dict(zip(SCATTER_ORDERS[color], where))
         return (*(at[axis] for axis in AXES), slice(*SHARES[color]))
-
-    STARTS = (0, 2, 4, 6, 8, 11)
 
     def copy(self, color, slot):
         a, b, c = SCATTER_ORDERS[color]
@@ -163,15 +165,15 @@
         k = slot - self.STARTS[stage]
         step, half = STEPS[k], pl.ds(2 * k, 2)
         if stage == 0:
-            src, dst, axis = self.mine.at[self.term(color, (p.along(a, 2), half, EVERY))], self.in_h[color].at[k], a
+            src, dst, axis = self.mine.at[self.term(color, (p.along(a, 2), half, EVERY))], self.in_h[color].at[twin, k], a
         elif stage == 1:
-            src, dst, axis = self.mine.at[self.term(color, (p.along(a, step), EVERY, EVERY))], self.in_a[color].at[k], a
+            src, dst, axis = self.mine.at[self.term(color, (p.along(a, step), EVERY, EVERY))], self.in_a[color].at[twin, k], a
         elif stage == 2:
-            src, dst, axis = self.send_b[color].at[twin, p.along(b, 2), half], self.in_bh[color].at[k], b
+            src, dst, axis = self.send_b[color].at[p.along(b, 2), half], self.in_bh[color].at[k], b
         elif stage == 3:
-            src, dst, axis = self.send_b[color].at[twin, p.along(b, step)], self.in_b[color].at[k], b
+            src, dst, axis = self.send_b[color].at[p.along(b, step)], self.in_b[color].at[k], b
         else:
-            src, dst, axis = self.send_c[color].at[twin, p.along(c, step)], self.in_c[color].at[self.number, k], c
+            src, dst, axis = self.send_c[color].at[p.along(c, step)], self.in_c[color].at[self.number, k], c
         return remote(src, dst, *sems, p.peer(axis, step))
 
     def stage(self, number):
@@ -182,7 +184,8 @@
             self.sum(number, color, *axes)
             for slot in range(self.STARTS[number], self.STARTS[number + 1]) if number < last else ():
                 self.copy(color, slot).start()
-            for slot in range(self.STARTS[2], self.STARTS[last]) if number == last else ():
+            done = {3: self.STARTS[:3:2], last: self.STARTS[2::3]}.get(number)
+            for slot in range(*done) if done else ():
                 self.copy(color, slot).wait_send()
 
     def sum(self, number, color, a, b, c):
@@ -199,7 +202,7 @@
                 def _(k):
                     i, j = k // RING, k % RING
                     at = self.term(color, (p.along(a, step), 2 * slot + i, j))
-                    mine[at] = (mine[at].astype(F32) + in_h[(slot, *flip(i, j))].astype(F32)).astype(BF)
+                    mine[at] = (mine[at].astype(F32) + in_h[(twin, slot, *flip(i, j))].astype(F32)).astype(BF)
 
         if number == 2:
 
@@ -207,9 +210,10 @@
             def _(k):
                 i, j = k // RING, k % RING
                 total = mine[self.term(color, (p.at[a], i, j))].astype(F32)
-                total = total + in_a[(0, *flip(i, j))].astype(F32) + in_a[(1, *flip(i, j))].astype(F32)
+                for slot, _ in SIDES:
+                    total = total + in_a[(twin, slot, *flip(i, j))].astype(F32)
                 acc_b[i, j] = total
-                send_b[twin, i, j] = total.astype(BF)
+                send_b[i, j] = total.astype(BF)
 
         if number == 3:
             for slot, step in SIDES:
@@ -217,30 +221,25 @@
 
                 @pl.loop(0, 2)
                 def _(j):
-                    send_b[twin, i, 2 * slot + j] = (acc_b[i, 2 * slot + j] + in_bh[slot, j].astype(F32)).astype(BF)
+                    send_b[i, 2 * slot + j] = (acc_b[i, 2 * slot + j] + in_bh[slot, j].astype(F32)).astype(BF)
 
         if number == 4:
 
             @pl.loop(0, RING)
             def _(j):
-                total = acc_b[p.at[b], j] + in_b[0, j].astype(F32) + in_b[1, j].astype(F32)
+                total = acc_b[p.at[b], j]
+                for slot, _ in SIDES:
+                    total = total + in_b[slot, j].astype(F32)
                 acc_c[j] = total
-                send_c[twin, j] = total.astype(BF)
+                send_c[j] = total.astype(BF)
 
         if number == 5:
             total = acc_c[p.at[c]]
             for slot in AXES:
                 total = total + in_c[self.number, slot].astype(F32)
             lo, hi = SHARES[color]
-            high = self.out.shape[0] // ROWS
             for k in range(lo, hi):
-                col, row = k // high, k % high
-                self.out[pl.ds(ROWS * row, ROWS), pl.ds(LANES * col, LANES)] = total[k - lo].astype(BF)
-
-    def finish(self):
-        for color in AXES:
-            for slot in range(self.STARTS[2]):
-                self.copy(color, slot).wait_send()
+                self.put(k, total[k - lo])
 
 
 def scatter_scratch(jobs):
@@ -249,20 +248,34 @@
     for (lo, hi), (a, b, c) in zip(SHARES, SCATTER_ORDERS):
         half = two + ring if b < c else ring + two
         shapes = (
-            (two + ring + ring, BF), (two + half, BF), (ring + ring, F32), (two + ring + ring, BF), (two + ring, BF), (two + two, BF), (ring, F32),
-            (two + ring, BF), ((jobs, len(STEPS)), BF),
+            (two + two + ring + ring, BF), (two + two + half, BF), (ring + ring, F32), (ring + ring, BF), (two + ring, BF), (two + two, BF),
+            (ring, F32), (ring, BF), ((jobs, len(STEPS)), BF),
         )
-        groups.append([pltpu.VMEM((*shape, hi - lo, ROWS, LANES), kind) for shape, kind in shapes])
+        groups.append([pltpu.VMEM((*shape, hi - lo, PAIR, LANES), kind) for shape, kind in shapes])
     return zip(*groups)
 
 
-def store_tiles(val, store, high):
-    for k in range(val.shape[1] // LANES):
-        store(k, val[:, LANES * k : LANES * (k + 1)].reshape(-1, high, ROWS, LANES).astype(BF))
+def put_gate_up(out):
+    def put(k, unit):
+        out[:, part(k, LANES)] = unit.astype(BF)
+
+    return put
+
+
+def put_down(out):
+    def put(k, unit):
+        extra = k - D // LANES * 2
+        if extra < 0:
+            out[part(k % 2, PAIR), part(k // 2, LANES)] = unit.astype(BF)
+        else:
+            for n in range(2):
+                out[part(HIGH - 1, ROWS), part(2 * extra + n, LANES)] = unit[ROWS * n : ROWS * (n + 1)].astype(BF)
+
+    return put
 
 
 def part(k, size):
-    return pl.ds(pl.multiple_of(k * size, size), size)
+    return slice(k * size, (k + 1) * size) if isinstance(k, int) else pl.ds(pl.multiple_of(k * size, size), size)
 
 
 def blocks(shape, places, **mode):
@@ -416,7 +429,7 @@
 
 def forward(wg, wu, wd, x, dy):
     layers, rows = wg.shape[:-1]
-    high = TILES * LANES // D
+    high = HIGH
     outs = [
         shaped(layers, 2, *CUBE, rows, FF), shaped(layers, *CUBE, high, ROWS, D), shaped(D, T), shaped(2, T, FF, kind=F32), shaped(T, FF),
         shaped(T, D), shaped(D, T), shaped(T, FF), shaped(2, T, FF),
@@ -428,159 +441,160 @@
     return call(wg, wu, wd.reshape(layers, high, ROWS, D), x, dy)
 
 
-def down_grad(act, by_out, sink, hooks, outs=(), out_specs=()):
-    high = TILES * LANES // D
-
-    def body(act_cols, *refs):
+def down_grad(act, by_out, mine, hooks):
+    def body(act_cols):
         k = pl.program_id(0)
         at_step(hooks, k)
-
-        def store(c, val):
-            sink(k, slice(high * c, high * (c + 1)), val.reshape(RING, RING, high, ROWS, LANES), *refs)
-
-        store_tiles(dot(act_cols[...], by_out[...], 0, 0), store, high)
-
-    pltpu.emit_pipeline(body, grid=(RING,), in_specs=[blocks((T, FF // RING), {1: 0})], out_specs=list(out_specs))(act, *outs)
+        val = dot(act_cols[...], by_out[...], 0, 0)
+        tiles = D // LANES
+        left = None
+        for c in range(tiles):
+            col = val[:, part(c, LANES)].reshape(RING**2, HIGH, ROWS, LANES)
+            mine[k, :, :, 2 * c : 2 * c + 2] = col[:, : HIGH - 1].reshape(RING, RING, 2, PAIR, LANES).astype(BF)
+            last = col[:, HIGH - 1 :]
+            if c % 2:
+                both = jnp.concatenate([left, last], 1).reshape(RING, RING, PAIR, LANES)
+                mine[k, :, :, 2 * tiles + c // 2] = both.astype(BF)
+            left = last
+
+    pltpu.emit_pipeline(body, grid=(RING,), in_specs=[blocks((T, FF // RING), {1: 0})])(act)
 
 
 def gate_up_grads(a_t, dgu, mine, hooks):
-    high = TILES * LANES // FF
     wide = 512
     each = FF // wide
 
     def body(cols):
         k = pl.program_id(0)
         at_step(hooks, k)
-
-        def store(c, val):
-            tiles = pl.ds((k % each) * (high * wide // LANES) + high * c, high)
-            mine[1 + k // each, :, :, :, tiles] = val.reshape(*CUBE, high, ROWS, LANES)
-
-        store_tiles(dot(a_t[...], cols[...]), store, high)
+        val = dot(a_t[...], cols[...])
+        for c in range(wide // LANES):
+            col = val[:, part(c, LANES)].reshape(*CUBE, PAIR, LANES).astype(BF)
+            mine[1 + k // each, :, :, :, (k % each) * (wide // LANES) + c] = col
 
     pltpu.emit_pipeline(body, grid=(2 * each,), in_specs=[pl.BlockSpec((None, T, wide), lambda k: (k // each, 0, k % each))])(dgu)
 
 
-def state_grad(dgu, w, h, by_out, out, keep, hooks):
-    def body(d, h, out):
-        k = pl.program_id(0)
-        at_step(hooks, k)
-        rows = part(k, MXU)
+def state_grad(dgu, w, h, by_out, held, out, keep, hooks):
+    steps = T // MXU
+
+    def project(d, k):
         by_gate, by_up = (dot(d[m], w[m], 1, 1).astype(BF).astype(F32) for m in range(2))
-        by_a = (by_gate + by_up).astype(BF).astype(F32)
+        held[k % 2] = (by_gate + by_up).astype(BF)
+
+    def finish(h, outs, k):
+        rows = part(jnp.maximum(k - 1, 0), MXU)
+        by_a = held[(k + 1) % 2].astype(F32)
         wide = h[...].astype(F32)
         scale = lax.rsqrt(jnp.mean(wide**2, -1, keepdims=True) + 1e-6)
         inner = jnp.mean(by_a * wide, -1, keepdims=True)
         by_norm = (by_a * scale - wide * (inner * scale * scale * scale)).astype(BF)
         total = (by_out[rows].astype(F32) + by_norm.astype(F32)).astype(BF)
-        out[...] = total
-        if keep is not None:
+        if keep is None:
+            outs[0][...] = total
+        else:
             keep[rows] = total
 
-    rows = blocks((MXU, D), {0: 0})
-    pltpu.emit_pipeline(body, grid=(T // MXU,), in_specs=[blocks((2, MXU, FF), {1: 0}), rows], out_specs=[rows])(dgu, h, out)
-
-
-def scatter_jobs(place, mine, outs, bufs, send, recv):
-    groups = [bufs[k : k + len(SHARES)] for k in range(0, len(bufs), len(SHARES))]
-    return [Scatter(place, mine.at[k], out, k, groups, send.at[k], recv.at[k]) for k, out in enumerate(outs)]
-
-
-def at_slot(jobs, t):
-    return slots(*((job, t - 2 * k) for k, job in enumerate(jobs) if 0 <= t - 2 * k < len(Scatter.STARTS)))
-
-
-def rest_of(jobs, first):
-    for t in range(first, len(Scatter.STARTS) + 2 * (len(jobs) - 1)):
-        at_slot(jobs, t)()
-    for job in jobs:
-        job.finish()
-
-
-def second_kernel(act2, dy, aT1, dgu2, w2, h1, act1, dh1, down1, d_out, g_out, u_out, dy_v, t_v, dh_v, w_v, mine, *more):
-    *bufs, sem, send, recv = more
-    place = Place()
-    loads = [pltpu.make_async_copy(*pair, sem.at[k]) for k, pair in enumerate(((dy, dy_v), (aT1, t_v), (w2.at[1], w_v)))]
-    for copy in loads:
-        copy.start()
-    enter(place, 0)
-    jobs = scatter_jobs(place, mine, (d_out, g_out, u_out), bufs, send, recv)
-    load_dy, load_t, load_w = loads
-    load_dy.wait()
-
-    def keep_down(k, tiles, val):
-        mine[0, k, :, :, tiles] = val
-
-    down_grad(act2, dy_v, keep_down, {})
-    load_t.wait()
-    gate_up_grads(t_v, dgu2, mine, {0: at_slot(jobs, 0), 4: at_slot(jobs, 1), 9: at_slot(jobs, 2)})
-    load_w.wait()
-    state_grad(dgu2, w_v, h1, dy_v, dh1, dh_v, {2: at_slot(jobs, 3), 6: at_slot(jobs, 4)})
-
-    def put_down(k, tiles, val, out):
-        out[:, :, tiles] = val
-
-    down_grad(act1, dh_v, put_down, {1: at_slot(jobs, 5)}, [down1], [blocks((None, *down1.shape[1:]), {0: 0})])
-    rest_of(jobs, 6)
-
-
-SUMS = [((TILES * LANES // D * ROWS, D), VM), ((TILES * LANES // FF * ROWS, FF), VM), ((TILES * LANES // FF * ROWS, FF), VM)]
-
-
-def scatter_scratch_all():
-    return [
-        pltpu.VMEM((len(SUMS), *CUBE, TILES, ROWS, LANES), BF),
-        *(buf for group in scatter_scratch(len(SUMS)) for buf in group),
-        pltpu.SemaphoreType.DMA((4,)),
-        *[pltpu.SemaphoreType.DMA((len(SUMS), len(SHARES), Scatter.STARTS[-1]))] * 2,
-    ]
-
-
-def backward(kernel, number, outs, vmem, args):
-    outs = [(t, ANY) for t in outs] + [(shaped(*shape), spec) for shape, spec in SUMS]
-    return calls(kernel, number, [ANY] * len(args), outs, [pltpu.VMEM(t, BF) for t in vmem] + scatter_scratch_all())(*args)
-
-
-def second(*args):
-    outs = [shaped(T, D), shaped(*CUBE, TILES, ROWS, LANES)]
-    return backward(second_kernel, 1, outs, [(T, D), (D, T), (T, D), (2, D, FF)], args)
-
-
-def first_kernel(dh1, gate_up, wd1, aT0, w1, x, down1, dx, dgu1, d_out, g_out, u_out, dh_v, t_v, wd_v, w_v, mine, *more):
-    *bufs, sem, send, recv = more
-    place = Place()
-    pairs = ((down1, mine.at[0]), (dh1, dh_v), (wd1.at[0], wd_v), (aT0, t_v))
-    loads = [pltpu.make_async_copy(*pair, sem.at[k]) for k, pair in enumerate(pairs)]
-    for copy in loads:
-        copy.start()
-    enter(place, 0)
-    jobs = scatter_jobs(place, mine, (d_out, g_out, u_out), bufs, send, recv)
-    for copy in loads:
-        copy.wait()
-    load_w = pltpu.make_async_copy(w1.at[0], w_v, sem.at[0])
-    load_w.start()
-    at_slot(jobs, 0)()
-    hooks = {10: at_slot(jobs, 1)}
+    def body(d, h, *outs):
+        k = pl.program_id(0)
+        at_step(hooks, k)
+
+        @pl.when(k < steps)
+        def _():
+            finish(h, outs, k)
+            project(d, k)
+
+        pl.when(k == steps)(lambda: finish(h, outs, k))
+
+    behind = pl.BlockSpec((MXU, D), lambda k: (jnp.maximum(k - 1, 0), 0))
+    pltpu.emit_pipeline(
+        body,
+        grid=(steps + 1,),
+        in_specs=[pl.BlockSpec((2, MXU, FF), lambda k: (0, jnp.minimum(k, steps - 1), 0)), behind],
+        out_specs=[behind] if keep is None else [],
+    )(dgu, h, *([out] if keep is None else []))
+
+
+def act_grads(gate_up, by_out, w, out, hooks):
     wide = 512
 
-    def act_body(gu, out):
+    def body(gu, out):
         col, row = pl.program_id(0), pl.program_id(1)
         at_step(hooks, col * (T // wide) + row)
-        by_act = dot(dh_v[part(row, wide)], wd_v[part(col, wide)], 1, 1).astype(BF).astype(F32)
+        by_act = dot(by_out[part(row, wide)], w[part(col, wide)], 1, 1).astype(BF).astype(F32)
         silu, slope = silu_parts(gu[0])
         for m, val in enumerate((by_act * gu[1] * slope, by_act * silu)):
             out[m] = val.astype(BF)
 
     block = blocks((2, wide, wide), {1: 1, 2: 0})
-    pltpu.emit_pipeline(act_body, grid=(FF // wide, T // wide), in_specs=[block], out_specs=[block])(gate_up, dgu1)
-    gate_up_grads(t_v, dgu1, mine, {5: at_slot(jobs, 2), 9: at_slot(jobs, 3)})
+    pltpu.emit_pipeline(body, grid=(FF // wide, T // wide), in_specs=[block], out_specs=[block])(gate_up, out)
+
+
+PHASES = (
+    {},
+    {0: [(0, 0)], 3: [(0, 1)], 5: [(1, 0)], 7: [(0, 2)], 9: [(0, 3)]},
+    {0: [(1, 1), (2, 0)], 1: [(0, 4)], 3: [(0, 5)], 4: [(1, 2)], 6: [(1, 3)], 7: [(2, 1)]},
+    {0: [(1, 4)], 1: [(1, 5)], 3: [(2, 2)]},
+    {0: [(2, 3), (3, 0)], 5: [(2, 4)], 9: [(2, 5), (3, 1)]},
+    {0: [(3, 2)], 1: [(3, 3)], 3: [(3, 4)], 4: [(3, 5)], 5: [(4, 0)], 8: [(4, 1)]},
+    {0: [(5, 0)], 2: [(4, 2)], 3: [(4, 3)], 4: [(5, 1)], 5: [(4, 4)], 6: [(4, 5)]},
+)
+ENDING = ((5, 2), (5, 3), (5, 4), (5, 5))
+
+
+def backward_kernel(
+    act2, dy, aT1, dgu2, gu_w, h1, act1, gate_up, d_w, aT0, x, dx, dgu1, d_out, g_out, u_out, dy_w_v, t_v, dh_v, w_v, held, mine, *more
+):
+    *bufs, sem, send, recv = more
+    place = Place()
+    sems = [sem.at[k] for k in range(sem.shape[0])]
+
+    def load(src, dst):
+        copy = pltpu.make_async_copy(src, dst, sems.pop())
+        copy.start()
+        return copy
+
+    dy_v = dy_w_v.at[:T]
+    load_dy, load_t, load_w = load(dy, dy_v), load(aT1, t_v), load(gu_w.at[1], w_v)
+    enter(place, 0)
+    groups = [bufs[k : k + len(SHARES)] for k in range(0, len(bufs), len(SHARES))]
+    jobs = []
+    for layer in (1, 0):
+        for k, put in enumerate((put_down(d_out.at[layer]), put_gate_up(g_out.at[layer]), put_gate_up(u_out.at[layer]))):
+            n = len(jobs)
+            jobs.append(Scatter(place, mine.at[k], put, n, groups, send.at[n], recv.at[n]))
+    hooks = [{step: slots(*((jobs[n], stage) for n, stage in pairs)) for step, pairs in phase.items()} for phase in PHASES]
+    load_dy.wait()
+    down_grad(act2, dy_v, mine.at[0], hooks[0])
+    load_t.wait()
+    gate_up_grads(t_v, dgu2, mine, hooks[1])
+    load_t = load(aT0, t_v)
     load_w.wait()
-    state_grad(dgu1, w_v, x, dh_v, dx, None, {2: at_slot(jobs, 4), 5: at_slot(jobs, 5)})
-    rest_of(jobs, 6)
-
-
-def first(*args):
-    return backward(first_kernel, 2, [shaped(T, D), shaped(2, T, FF)], [(T, D), (D, T), (FF, D), (2, D, FF)], args)
+    state_grad(dgu2, w_v, h1, dy_v, held, None, dh_v, hooks[2])
+    load_w = load(gu_w.at[0], w_v)
+    load_d = load(d_w.at[0], dy_w_v)
+    down_grad(act1, dh_v, mine.at[0], hooks[3])
+    load_d.wait()
+    act_grads(gate_up, dh_v, dy_w_v, dgu1, hooks[4])
+    load_t.wait()
+    gate_up_grads(t_v, dgu1, mine, hooks[5])
+    load_w.wait()
+    state_grad(dgu1, w_v, x, dh_v, held, dx, None, hooks[6])
+    slots(*((jobs[n], stage) for n, stage in ENDING))()
+
+
+def backward(*args):
+    n = 6
+    sums = [shaped(2, HIGH * ROWS, D), shaped(2, PAIR, FF), shaped(2, PAIR, FF)]
+    outs = [(shaped(T, D), ANY), (shaped(2, T, FF), ANY)] + [(t, VM) for t in sums]
+    vmem = [(FF, D), (D, T), (T, D), (2, D, FF), (2, MXU, D), (len(sums), *CUBE, UNITS, PAIR, LANES)]
+    scratch = [
+        *(pltpu.VMEM(t, BF) for t in vmem),
+        *(buf for group in scatter_scratch(n) for buf in group),
+        pltpu.SemaphoreType.DMA((n,)),
+        *[pltpu.SemaphoreType.DMA((n, len(SHARES), Scatter.STARTS[-1]))] * 2,
+    ]
+    return calls(backward_kernel, 1, [ANY] * len(args), outs, scratch)(*args)
 
 
 def solution(mesh):
@@ -588,9 +602,8 @@
         x, dy = x[0], dy[0]
         gu, down, aT0, gate_up, act1, h1, aT1, act2, dgu2 = forward(wg, wu, wd, x, dy)
         gu, down = gu.reshape(-1, 2, D, FF), down.reshape(-1, FF, D)
-        dh1, down1, d2, g2, u2 = second(act2, dy, aT1, dgu2, gu, h1, act1)
-        dx, _, d1, g1, u1 = first(dh1, gate_up, down, aT0, gu, x, down1)
-        return dx[None], jnp.stack([g1, g2]), jnp.stack([u1, u2]), jnp.stack([d1, d2])
+        dx, _, by_d, by_g, by_u = backward(act2, dy, aT1, dgu2, gu, h1, act1, gate_up, down, aT0, x)
+        return dx[None], by_g, by_u, by_d
 
     seq, rows = P(("rep", "dp"), None, None), P(None, "dp", None)
     return jax.shard_map(

time: 387 us -> 383 us (0.990)
  Pallas kernels: 377 us -> 372 us
  local copies, waits for them, and re-layouts: 4.65 us -> 9.42 us
    pallas_call x2 -> x1, Pallas kernels: 233 us -> 228 us  [backward(): return calls(backward_kernel, 1, [ANY] * len(args), outs, scratch)(*args)]
    unnamed x7 -> x4, local copies, waits for them, and re-layouts: 4.65 us -> 9.42 us
where the time goes in v3:
time: 383 us; the launch traced here: 382 us
  Pallas kernels  372 us (97%)
  local copies, waits for them, and re-layouts  9.42 us (2%)
    pallas_call x1, Pallas kernels, backward(): return calls(backward_kernel, 1, [ANY] * len(args), outs, scratch)(*args)  228 us
    pallas_call x1, Pallas kernels, forward(): return call(wg, wu, wd.reshape(layers, high, ROWS, D), x, dy)  144 us
    unnamed x4, local copies, waits for them, and re-layouts  9.42 us

profile of v3, /device:TPU:0, one launch (start us, length us, event | category | flops | bytes accessed | tf_op | source)
XLA Modules:
  0.0 382.3 jit_solution(18126541832990356126)
XLA Ops:
  0.6 144.2 %forward_kernel.1 = (bf16[2,2,4,4,4,16,2560]{6,5,4,3,2,1,0:T(8,128)(2,1)}, bf16[2,4,4,4,5,8,1024]{6,5,4,3,2,1,0:T(8,128)(2,1)}, bf16[1024,2048]{1,0:T(8,128)(2,1...) custom-call(bf16[2,16,2560]{2,1,0:T(8,128)(2,1)} %g_ref.1, ...), custom_call_target="tpu_custom_call" | custom-call | tf_op jit(solution)/shard_map/forward_kernel/pallas_call | solution.py:441
  144.8 228.1 %backward_kernel.1 = (bf16[2048,1024]{1,0:T(8,128)(2,1)}, bf16[2,2048,2560]{2,1,0:T(8,128)(2,1)}, bf16[2,40,1024]{2,1,0:T(8,128)(2,1)}, bf16[2,16,2560]{2,1,0:T(8,128)(2,1)}, bf16[2,16,2560]{2,1,0:T(8,128)(2,1)}) custom-call(bf16[2048,2560]{1,0:T(8,128)(2,1)} %get-tuple-element.17.act2, bf16[2048,1024]{1,0:T(8,128)(2,1)} %bitcast.10, ...), custom_call_target="tpu_custom_call" | custom-call | tf_op jit(solution)/shard_map/backward_kernel/pallas_call | solution.py:597
  372.9 4.6 %copy.13 = bf16[1,2048,1024]{2,1,0:T(8,128)(2,1)} copy(bf16[1,2048,1024]{2,1,0:T(8,128)(2,1)} %bitcast.12) | data formatting | bytes 8388608
  377.5 1.6 copy.14
  379.1 1.6 copy.15
  380.7 1.6 copy.16
